TPU v7x, 256 devices: a whole 4x4x8 slice. The times are simulated.
256 devices in a mesh: dp: 32 (over y, z), tensor: 8 (over x, core).
Axes of the slice: x: 4, y: 4, z: 8, core: 2. Of those that a mesh axis runs over, the one named last changes fastest.
Arguments:
- qkv: bfloat16 [3, 16384, 4096], P(None, 'dp', 'tensor'), may hold values from -6 to 6
- segment_ids: int32 [32, 8, 64], P('dp'), may hold values from 0 to 1, never falling along the last dimension, each value on 1 to 63 neighbouring positions
- out_weight: bfloat16 [4096, 4096], P(None, 'tensor'), may hold values from -0.09375 to 0.09375
- out_bias: bfloat16 [4096], replicated, may hold values from -3 to 3
- upstream: bfloat16 [16384, 4096], P(('dp', 'tensor')), may hold values from -24 to 24
- pre_act: bfloat16 [16384, 8192], P('dp', 'tensor'), may hold values from -6 to 6
- down_weight: bfloat16 [4096, 8192], P('dp', 'tensor'), may hold values from -0.0625 to 0.0625
Outputs:
- attention_out: float32 [16384, 4096], P(('dp', 'tensor'))
- act_grad: float32 [16384, 8192], P('dp', 'tensor')
- weight_grad: float32 [4096, 8192], P('dp', 'tensor')
Inputs may be any that keep to these rules, and one draw needn't show every extreme that they name: `segment_ids`: within each pack the ids never fall; 2 images a pack, each of 1 to 63 tokens.
All inputs are finite; a program needn't handle non-finite values.
Results may differ from a plain program's by a relative error of at most 0.0055.
Values may be sent and summed in bfloat16 or wider, within the bound.
A program may use at most 128 MiB of HBM per device.

v0:
```python
import math

import jax
import jax.numpy as jnp
from jax import lax
from jax.sharding import Mesh
from jax.sharding import PartitionSpec as P

HEAD = 128
ROWS_DEV = 64
DP = ("dp_0", "dp_1")
DP_TENSOR = ("dp_0", "dp_1", "tensor")


root_half = 1.0 / math.sqrt(2.0)
inv_root_tau = 1.0 / math.sqrt(2.0 * math.pi)


def in_blocks(shard, dim, devices):
    lengths = shard.shape
    parts = shard.reshape(*lengths[:dim], devices, lengths[dim] // devices, *lengths[dim + 1 :])
    return jnp.moveaxis(parts, dim, 0)


def summed_on_arrival(shard, axis, dim):
    devices = lax.axis_size(axis)
    parts = lax.all_to_all(in_blocks(shard, dim, devices), axis, 0, 0, tiled=True)
    return jnp.sum(parts.astype(jnp.float32), axis=0)


def summed_rows(so_far, axes):
    for axis in axes:
        so_far = lax.psum_scatter(so_far, axis, scatter_dimension=0, tiled=True)
    return so_far


def gelu_exact(argument):
    return 0.5 * argument * (1.0 + lax.erf(argument * root_half))


def gelu_slope(argument):
    return (
        0.5 * (1.0 + lax.erf(argument * root_half))
        + argument * jnp.exp(-0.5 * argument * argument) * inv_root_tau
    )


def attend(qkv, labels):
    length = qkv.shape[1]
    head_count = qkv.shape[2] // HEAD
    queries = qkv[0].reshape(length, head_count, HEAD)
    key_rows = qkv[1].reshape(length, head_count, HEAD)
    value_rows = qkv[2].reshape(length, head_count, HEAD)
    scores = jnp.einsum("qhd,khd->hqk", queries, key_rows, preferred_element_type=jnp.float32) * (
        1.0 / math.sqrt(HEAD)
    )
    pack_of = jnp.arange(length, dtype=jnp.int32) // ROWS_DEV
    same_image = ((labels[:, None] == labels[None, :]) & (pack_of[:, None] == pack_of[None, :]))[
        None
    ]
    masked = jnp.where(same_image, scores, -1e30)
    row_top = jnp.max(masked, axis=2, keepdims=True)
    exponent = jnp.where(same_image, jnp.exp(masked - row_top), 0.0)
    weights = (exponent / jnp.sum(exponent, axis=2, keepdims=True)).astype(jnp.bfloat16)
    context = jnp.einsum("hqk,khd->qhd", weights, value_rows, preferred_element_type=jnp.float32)
    return context.reshape(length, head_count * HEAD).astype(jnp.bfloat16)


def body(qkv, segment_ids, out_weight, out_bias, upstream, pre_act, down_weight):
    context = attend(qkv, segment_ids[0].reshape(-1))
    summed = summed_on_arrival(
        lax.dot_general(
            context, out_weight, (((1,), (1,)), ((), ())), preferred_element_type=jnp.float32
        ).astype(jnp.bfloat16),
        "tensor",
        0,
    )
    attention_out = summed + out_bias.astype(jnp.float32)
    whole_grad = lax.all_gather(upstream, "tensor", axis=0, tiled=True)
    columns = whole_grad
    hidden_grad = jnp.dot(
        columns,
        lax.all_gather(down_weight, DP, axis=0, tiled=True),
        preferred_element_type=jnp.float32,
    )
    preact = pre_act.astype(jnp.float32)
    act_grad = hidden_grad * gelu_slope(preact)
    activation = gelu_exact(preact).astype(jnp.bfloat16)
    factor = 1.0 / lax.axis_size(DP)
    columns = whole_grad
    product = lax.dot_general(
        columns, activation, (((0,), (0,)), ((), ())), preferred_element_type=jnp.float32
    )
    weight_grad = summed_rows(product * factor, DP)
    return (attention_out, act_grad, weight_grad)


def solution(mesh):
    finer = Mesh(mesh.devices.reshape(4, 8, mesh.shape["tensor"]), ("dp_0", "dp_1", "tensor"))
    in_specs = (
        P(None, DP, "tensor"),
        P(DP, None, None),
        P(None, "tensor"),
        P(),
        P(DP_TENSOR, None),
        P(DP, "tensor"),
        P(DP, "tensor"),
    )
    out_specs = (P(DP_TENSOR, None), P(DP, "tensor"), P(DP, "tensor"))
    return jax.shard_map(body, mesh=finer, in_specs=in_specs, out_specs=out_specs, check_vma=False)
```

profile of v0, /device:TPU:1, one launch (start us, length us, event | category | flops | bytes accessed | tf_op | source)
XLA Modules:
  0.0 341.7 jit_solution(4733892709026536112)
XLA Ops:
  8.0 0.7 all-gather.3.cloned.1.call-update
  8.8 40.7 %all-gather.3.cloned.1.call-done = bf16[512,4096]{1,0:T(8,128)(2,1)} async-done(((bf16[64,4096]{1,0:T(8,128)(2,1)}), bf16[512,4096]{1,0:T(8,128)(2,1)}) %all-gather.3.cloned.1.call-update) | async-done | bytes 4194320 | tf_op jit(solution)/shard_map/all_gather | solution.py:79
  49.5 12.8 %multiply_bitcast_fusion = f32[4096,1024]{0,1:T(8,128)} fusion(bf16[512,4096]{1,0:T(8,128)(2,1)} %all-gather.3.cloned.1.call-done, bf16[512,1024]{1,0:T(8,128)(2,1)} %param.12), kind=kOutput, calls=%fused_computation.1 | convolution fusion | flops 4302307328 | bytes 22020096 | tf_op jit(solution)/shard_map/dot_general | solution.py:91
  62.3 0.0 all-gather.5.cloned.1.call-start
  62.4 0.5 all-gather.5.cloned.1.call-update
  62.9 0.0 reduce-scatter.5.cloned.1.call-start
  63.0 0.7 copy-done
  63.7 0.1 fusion.26
  63.8 186.6 %reduce-scatter.3.cloned.1.call-done = f32[1024,1024]{0,1:T(8,128)} async-done(((f32[4096,1024]{0,1:T(8,128)}), f32[1024,1024]{0,1:T(8,128)}) %reduce-scatter.3.cloned.1.call-update) | async-done | bytes 4194320 | tf_op jit(solution)/shard_map/reduce_scatter | solution.py:33
  250.5 0.1 eq.36
  250.6 0.2 copy.24
  250.8 0.2 copy.23
  251.0 0.2 copy.17
  251.2 0.3 compare_and_fusion
  251.5 4.0 %fusion.27 = (f32[4,512]{1,0:T(4,128)S(1)}, f32[4,512,512]{1,2,0:T(8,128)}) fusion(pred[512,512]{0,1:T(8,128)(4,1)S(1)} %compare_and_fusion, bf16[512,4,128]{0,2,1:T(8,128)(2,1)S(1)} %bitcast.22, bf16[512,4,128]{0,2,1:T(8,128)(2,1)S(1)} %bitcast.20), kind=kOutput, calls=%fused_computation.41 | convolution fusion | flops 273678848 | bytes 5513216 | tf_op jit(solution)/shard_map/sub | solution.py:63
  255.5 2.8 fusion.14
  258.4 0.6 copy-done.3
  259.0 4.4 %convolution_convert_fusion = bf16[512,4096]{1,0:T(8,128)(2,1)} fusion(bf16[512,512]{0,1:T(8,128)(2,1)S(1)} %bitcast.23, bf16[4096,512]{1,0:T(8,128)(2,1)S(1)} %copy-done.3), kind=kOutput, calls=%fused_computation.3 | convolution fusion | flops 2149580800 | bytes 8912896 | tf_op jit(solution)/shard_map/dot_general | solution.py:72
  263.4 5.3 %all-to-all-start = ((bf16[8,64,4096]{2,1,0:T(8,128)(2,1)}), bf16[8,64,4096]{2,1,0:T(8,128)(2,1)}, u32[]{:S(2)}, u32[]{:S(2)}) async-start(bf16[8,64,4096]{2,1,0:T(8,128)(2,1)} %bitcast.19), calls=%async_computation | async-start | bytes 8388608 | tf_op jit(solution)/shard_map/all_to_all | solution.py:27
  268.7 48.8 %all-to-all-done = bf16[8,64,4096]{2,1,0:T(8,128)(2,1)} async-done(((bf16[8,64,4096]{2,1,0:T(8,128)(2,1)}), bf16[8,64,4096]{2,1,0:T(8,128)(2,1)}, u32[]{:S(2)}, u32[]{:S(2)}) %all-to-all-start) | async-done | bytes 4194336 | tf_op jit(solution)/shard_map/all_to_all | solution.py:27
  317.5 3.0 convert_reduce_fusion
  320.5 1.0 broadcast_add_fusion
  321.5 11.0 %fusion.7 = f32[512,1024]{1,0:T(8,128)} fusion(bf16[512,1024]{1,0:T(8,128)(2,1)S(1)} %copy-done.4, bf16[512,4096]{1,0:T(8,128)(2,1)} %all-gather.3.cloned.1.call-done, bf16[4096,1024]{1,0:T(8,128)(2,1)} %all-gather.5.cloned.1.call-done), kind=kOutput, calls=%fused_computation.18 | convolution fusion | flops 4300210176 | bytes 15728640 | tf_op jit(solution)/shard_map/dot_general | solution.py:81
  332.5 2.0 copy.19
  (16 shorter events, 0.1 us)
Async XLA Ops:
  8.0 41.5 %all-gather.3.cloned.1.call-start = ((), (), s32[]{:S(2)}) async-start(), calls=%async_computation.3 | async-start | bytes 4718592 | tf_op jit(solution)/shard_map/all_gather | solution.py:79
  8.7 241.7 %reduce-scatter.3.cloned.1.call-start = ((), (), s32[]{:S(2)}) async-start(), calls=%async_computation.5 | async-start | bytes 20971520 | tf_op jit(solution)/shard_map/reduce_scatter | solution.py:33
  62.3 1.4 copy-start
  62.3 188.2 %copy-start.2 = (s32[1,8,64]{2,1,0:T(8,128)S(1)}, s32[1,8,64]{2,1,0:T(8,128)}, u32[]{:S(2)}) copy-start(s32[1,8,64]{2,1,0:T(8,128)} %param.8) | copy-start | bytes 6148
  62.3 259.2 %all-gather.5.cloned.1.call-start = ((), (), s32[]{:S(2)}) async-start(), calls=%async_computation.4 | async-start | bytes 8650752 | tf_op jit(solution)/shard_map/all_gather | solution.py:83
  62.9 269.6 %reduce-scatter.5.cloned.1.call-start = ((), (), s32[]{:S(2)}) async-start(), calls=%async_computation.6 | async-start | bytes 4718592 | tf_op jit(solution)/shard_map/reduce_scatter | solution.py:33
  255.5 3.4 %copy-start.3 = (bf16[4096,512]{1,0:T(8,128)(2,1)S(1)}, bf16[4096,512]{1,0:T(8,128)(2,1)}, u32[]{:S(2)}) copy-start(bf16[4096,512]{1,0:T(8,128)(2,1)} %param.9) | copy-start | bytes 12582916
  263.4 5.3 %copy-start.1 = (bf16[4096]{0:T(1024)(128)(2,1)S(1)}, bf16[4096]{0:T(1024)(128)(2,1)}, u32[]{:S(2)}) copy-start(bf16[4096]{0:T(1024)(128)(2,1)} %param.10) | copy-start | bytes 24580
  263.4 54.1 %all-to-all-start = ((bf16[8,64,4096]{2,1,0:T(8,128)(2,1)}), bf16[8,64,4096]{2,1,0:T(8,128)(2,1)}, u32[]{:S(2)}, u32[]{:S(2)}) async-start(bf16[8,64,4096]{2,1,0:T(8,128)(2,1)} %bitcast.19), calls=%async_computation | async-start | bytes 8388608 | tf_op jit(solution)/shard_map/all_to_all | solution.py:27
  268.7 52.9 %copy-start.4 = (bf16[512,1024]{1,0:T(8,128)(2,1)S(1)}, bf16[512,1024]{1,0:T(8,128)(2,1)}, u32[]{:S(2)}) copy-start(bf16[512,1024]{1,0:T(8,128)(2,1)} %param.12) | copy-start | bytes 3145732
Sparse Core Ops, SparseCore 0:
  10.7 38.7 all-gather.2
  62.5 187.9 reduce-scatter.2
  253.0 55.0 reduce-scatter.4
Sparse Core Ops, SparseCore 1:
  65.4 145.1 all-gather.4
where the time goes:
time: 342 us
  waiting for transfers between devices  277 us (81%)
  matrix products  35 us (10%)
  between operations  15.3 us (4%)
  starting transfers between devices  5.46 us (2%)
  other arithmetic  4.32 us (1%)
  local copies, waits for them, and re-layouts  4.23 us (1%)
    reduce_scatter x2, waiting for transfers between devices, summed_rows(): so_far = lax.psum_scatter(so_far, axis, scatter_dimension=0, tiled=True)  187 us
    all_to_all x1, waiting for transfers between devices, summed_on_arrival(): lax.all_to_all(in_blocks(shard, dim, devices), axis, 0, 0, tiled=True)  48.8 us
    all_gather x1, waiting for transfers between devices, body(): whole_grad = lax.all_gather(upstream, 'tensor', axis=0, tiled=True)  40.7 us
    dot_general x1, matrix products, body(): lax.dot_general(columns, activation, (((0,), (0,)), ((), ())), preferred_...  12.8 us
    dot_general x1, matrix products, body(): jnp.dot(columns, lax.all_gather(down_weight, DP, axis=0, tiled=True), pre...  11 us
  transfers between devices with their start and end apart: 5, of which 3 were waited for; matrix products, arithmetic and copies ran while one was open for 8% of the time, Pallas kernels for 0%

commit v1 on v0

v1 whole, which is shorter than its diff:
```python
import functools
import math

import jax
import jax.numpy as jnp
from jax import lax
from jax.experimental import pallas as pl
from jax.experimental.pallas import tpu as pltpu
from jax.sharding import Mesh
from jax.sharding import PartitionSpec as P

HEAD = 128
DP = ("y", "z")
DP_TENSOR = ("y", "z", "x", "c")
BF = jnp.bfloat16
F32 = jnp.float32

ROOT_HALF = 1.0 / math.sqrt(2.0)
INV_ROOT_TAU = 1.0 / math.sqrt(2.0 * math.pi)
SCALE = 1.0 / math.sqrt(HEAD)


class Ids:
    def __init__(self):
        self.n = 0

    def take(self, count=1):
        first = self.n
        self.n += count
        return first


IDS = Ids()
U1 = IDS.take(4)
U2R, U2L = IDS.take(4), IDS.take(4)
U2FR, U2FL = IDS.take(4), IDS.take(4)
U2S = IDS.take(4)
WR, WL = IDS.take(4), IDS.take(4)
AR, AL = IDS.take(4), IDS.take(4)
ARF, ALF = IDS.take(4), IDS.take(4)
ATS = IDS.take(4)
ATH, ATF = IDS.take(2), IDS.take(2)
HHS, HFS = IDS.take(2), IDS.take(4)
GRS = IDS.take(16)
N_IDS = IDS.n

LOCAL = Ids()
L_QKV, L_SEG, L_OW, L_PRE, L_UP, L_W, L_BIAS = (LOCAL.take() for _ in range(7))
L_ATT, L_WG = LOCAL.take(), LOCAL.take()
L_ACT = LOCAL.take(4)
N_LOCAL = LOCAL.n


def kernel(
    qkv, seg, out_weight, bias, upstream, pre_act, down_weight,
    att_hbm, act_hbm, wg_hbm,
    qkv_v, seg_v, ow_v, bias_v, pre_v, slope_v, ug, wg, ag, ctx,
    att_p, att_r, att_h, att_f, att_o,
    hp, hh, hf, h0, acc, gs, gr, go,
    ssem, rsem, lsem,
):
    y, z, x, c = (lax.axis_index(name) for name in ("y", "z", "x", "c"))
    t = 2 * x + c
    yy = [lax.rem(y + d, 4) for d in range(4)]
    zz = [lax.rem(z + d, 8) for d in range(8)]
    xx = [lax.rem(x + d, 4) for d in range(4)]
    oc = 1 - c
    sent = []
    local = []

    def send(k, src, dst, **where):
        copy = pltpu.make_async_remote_copy(
            src_ref=src, dst_ref=dst, send_sem=ssem.at[k], recv_sem=rsem.at[k],
            device_id=where, device_id_type=pl.DeviceIdType.MESH,
        )
        copy.start()
        sent.append(copy)

    def arrived(k, dst, **where):
        pltpu.make_async_remote_copy(
            src_ref=dst, dst_ref=dst, send_sem=ssem.at[k], recv_sem=rsem.at[k],
            device_id=where, device_id_type=pl.DeviceIdType.MESH,
        ).wait_recv()

    def fetch(k, src, dst):
        copy = pltpu.make_async_copy(src, dst, lsem.at[k])
        copy.start()
        return copy

    got_pre = fetch(L_PRE, pre_act, pre_v)
    got_up = fetch(L_UP, upstream.at[:, pl.ds(pl.multiple_of(y * 1024, 1024), 1024)], ug.at[y, t])
    got_w = fetch(L_W, down_weight, wg.at[z])
    got_seg = fetch(L_SEG, seg, seg_v)
    got_qkv = fetch(L_QKV, qkv, qkv_v)
    got_bias = fetch(L_BIAS, bias, bias_v)
    got_ow = fetch(L_OW, out_weight, ow_v)

    barrier = pltpu.get_barrier_semaphore()
    peers = [{"y": yy[d]} for d in (1, 2, 3)] + [{"z": zz[d]} for d in (1, 7)]
    peers += [{"x": xx[d]} for d in (1, 3)] + [{"c": oc}]
    for peer in peers:
        pl.semaphore_signal(barrier, inc=1, device_id=peer, device_id_type=pl.DeviceIdType.MESH)
    pl.semaphore_wait(barrier, len(peers))

    got_w.wait()
    send(WR, wg.at[z], wg.at[z], z=zz[1])
    send(WL, wg.at[z], wg.at[z], z=zz[7])
    for d in (1, 3, 2):
        columns = pl.ds(pl.multiple_of(yy[d] * 1024, 1024), 1024)
        send(U1 + d, upstream.at[:, columns], ug.at[y, t], y=yy[d])
    got_up.wait()
    send(U2R, ug.at[y, t], ug.at[y, t], x=xx[1])
    send(U2L, ug.at[y, t], ug.at[y, t], x=xx[3])

    got_pre.wait()

    def gelu(q):
        def rows(i, carry):
            here = pl.ds(pl.multiple_of(q * 128 + i * 16, 16), 16)
            v = pre_v[here, :].astype(F32)
            tail = 1.0 + lax.erf(v * ROOT_HALF)
            ag[y, here, :] = (0.5 * v * tail).astype(BF)
            slope_v[here, :] = 0.5 * tail + v * jnp.exp(-0.5 * v * v) * INV_ROOT_TAU
            return carry

        lax.fori_loop(0, 8, rows, 0)
        part = pl.ds(q * 128, 128)
        send(AR + q, ag.at[y, part], ag.at[y, part], y=yy[1])
        send(AL + q, ag.at[y, part], ag.at[y, part], y=yy[3])

    def own_upstream(e):
        arrived(U1 + (4 - e), ug.at[yy[e], t], y=yy[e])
        send(U2R + e, ug.at[yy[e], t], ug.at[yy[e], t], x=xx[1])
        send(U2L + e, ug.at[yy[e], t], ug.at[yy[e], t], x=xx[3])

    t_left, t_right, t_far = 2 * xx[3] + c, 2 * xx[1] + c, 2 * xx[2] + c

    def upstream_from_left(e, forward):
        slot = ug.at[yy[e], t_left]
        arrived(U2R + e, slot, x=xx[3])
        if forward:
            send(U2FR + e, slot, slot, x=xx[1])

    def upstream_from_right(e, forward):
        slot = ug.at[yy[e], t_right]
        arrived(U2L + e, slot, x=xx[1])
        if forward:
            send(U2FL + e, slot, slot, x=xx[3])

    def weight_hop(s):
        from_left, from_right = zz[8 - s], zz[s]
        arrived(WR + s - 1, wg.at[from_left], z=zz[7])
        arrived(WL + s - 1, wg.at[from_right], z=zz[1])
        if s < 3:
            send(WR + s, wg.at[from_left], wg.at[from_left], z=zz[1])
            send(WL + s, wg.at[from_right], wg.at[from_right], z=zz[7])
        else:
            low, high = pl.ds(0, 64), pl.ds(64, 64)
            send(WR + s, wg.at[from_left, low], wg.at[from_left, low], z=zz[1])
            send(WL + s, wg.at[from_right, high], wg.at[from_right, high], z=zz[7])

    def act_from_left(q, forward):
        slot = ag.at[yy[3], pl.ds(q * 128, 128)]
        arrived(AR + q, slot, y=yy[3])
        if forward:
            send(ARF + q, slot, slot, y=yy[1])

    def act_from_right(q, forward):
        slot = ag.at[yy[1], pl.ds(q * 128, 128)]
        arrived(AL + q, slot, y=yy[1])
        if forward:
            send(ALF + q, slot, slot, y=yy[3])

    gelu(0)
    gelu(1)
    own_upstream(3)
    own_upstream(1)
    gelu(2)
    gelu(3)
    own_upstream(2)
    send(U2S, ug.at[:, t], ug.at[:, t], c=oc)
    weight_hop(1)

    got_seg.wait()
    got_qkv.wait()
    labels = seg_v[0].astype(F32)
    row_i = lax.broadcasted_iota(jnp.int32, (128, 1), 0)
    col_i = lax.broadcasted_iota(jnp.int32, (1, 128), 1)
    for pair in range(4):
        first = [
            (64.0 - jnp.sum(labels[2 * pair + p : 2 * pair + p + 1, :], axis=1, keepdims=True)).astype(jnp.int32)
            for p in range(2)
        ]

        def image(i):
            second_pack = i >= 64
            place = jnp.where(second_pack, i - 64, i)
            bound = jnp.where(second_pack, first[1], first[0])
            return jnp.where(second_pack, 2, 0) + jnp.where(place >= bound, 1, 0)

        same = image(row_i) == image(col_i)
        rows = pl.ds(pair * 128, 128)
        for h in range(4):
            cols = pl.ds(h * 128, 128)
            s = lax.dot_general(
                qkv_v[0, rows, cols], qkv_v[1, rows, cols], (((1,), (1,)), ((), ())),
                preferred_element_type=F32,
            ) * SCALE
            s = jnp.where(same, s, -1e30)
            e = jnp.where(same, jnp.exp(s - jnp.max(s, axis=1, keepdims=True)), 0.0)
            w = (e / jnp.sum(e, axis=1, keepdims=True)).astype(BF)
            ctx[rows, cols] = jnp.dot(w, qkv_v[2, rows, cols], preferred_element_type=F32).astype(BF)

    upstream_from_left(0, True)
    upstream_from_right(3, True)
    act_from_left(0, True)
    got_ow.wait()

    def project(n, carry):
        cols = pl.ds(pl.multiple_of(n * 512, 512), 512)
        part = lax.dot_general(
            ctx[...], ow_v[cols, :], (((1,), (1,)), ((), ())), preferred_element_type=F32
        )
        att_p[:, :, :, cols] = part.astype(BF).reshape(4, 2, 64, 512)
        return carry

    lax.fori_loop(0, 4, project, 0)
    weight_hop(2)
    act_from_left(1, True)
    lax.fori_loop(4, 8, project, 0)
    order = (2, 1, 3, 0)
    for e in order:
        send(ATS + e, att_p.at[xx[e], oc], att_r.at[xx[e]], c=oc)
    upstream_from_left(1, True)
    upstream_from_right(2, True)
    for e in (2, 3):
        upstream_from_left(e, False)
    for e in (0, 1):
        upstream_from_right(e, False)
    send(U2S + 1, ug.at[:, t_left], ug.at[:, t_left], c=oc)
    send(U2S + 2, ug.at[:, t_right], ug.at[:, t_right], c=oc)
    act_from_right(2, True)

    def chip_sum(e):
        arrived(ATS + e, att_r.at[xx[e]], c=oc)

        def rows(i, carry):
            here = pl.ds(pl.multiple_of(i * 16, 16), 16)
            both = att_p[xx[e], c, here, :].astype(F32) + att_r[xx[e], here, :].astype(F32)
            att_p[xx[e], c, here, :] = both.astype(BF)
            return carry

        lax.fori_loop(0, 4, rows, 0)

    chip_sum(2)
    for k, cols in enumerate((pl.ds(0, 2048), pl.ds(2048, 2048))):
        send(ATH + k, att_p.at[xx[2], c, :, cols], att_h.at[k], x=xx[1] if k == 0 else xx[3])
    weight_hop(3)
    act_from_right(3, True)
    for e in (1, 3):
        chip_sum(e)

    for e in (0, 1):
        arrived(U2FR + e, ug.at[yy[e], t_far], x=xx[3])
    for e in (3, 2):
        arrived(U2FL + e, ug.at[yy[e], t_far], x=xx[1])
    send(U2S + 3, ug.at[:, t_far], ug.at[:, t_far], c=oc)
    for k, dx in ((0, 0), (1, 3), (2, 1), (3, 2)):
        arrived(U2S + k, ug.at[:, 2 * xx[dx] + oc], c=oc)
    low, high = pl.ds(0, 64), pl.ds(64, 64)
    arrived(WR + 3, wg.at[zz[4], low], z=zz[7])
    arrived(WL + 3, wg.at[zz[4], high], z=zz[1])

    def hidden(d, store):
        def tile(n, carry):
            cols = pl.ds(pl.multiple_of(n * 256, 256), 256)
            store(
                cols,
                jnp.dot(
                    ug[yy[d]].reshape(512, 1024), wg[:, :, cols].reshape(1024, 256),
                    preferred_element_type=F32,
                ),
            )
            return carry

        lax.fori_loop(0, 4, tile, 0)

    def to_send(d):
        def store(cols, value):
            hp[d - 1, :, cols] = value.astype(BF)

        return store

    def to_keep(cols, value):
        h0[:, cols] = value

    top, bottom = pl.ds(0, 256), pl.ds(256, 256)
    hidden(2, to_send(2))
    send(HHS, hp.at[1, top], hh.at[0], y=yy[1])
    send(HHS + 1, hp.at[1, bottom], hh.at[1], y=yy[3])
    hidden(1, to_send(1))
    send(HFS, hp.at[0, bottom], hf.at[0, bottom], y=yy[1])
    hidden(3, to_send(3))
    send(HFS + 1, hp.at[2, top], hf.at[1, top], y=yy[3])

    for k, e, lo in ((0, 1, 0), (1, 3, 2048)):
        arrived(ATH + k, att_h.at[k], x=xx[3] if k == 0 else xx[1])

        def add_half(i, carry, k=k, e=e, lo=lo):
            here = pl.ds(pl.multiple_of(i * 16, 16), 16)
            cols = pl.ds(lo, 2048)
            total = att_p[xx[e], c, here, cols].astype(F32) + att_h[k, here, :].astype(F32)
            att_p[xx[e], c, here, cols] = total.astype(BF)
            return carry

        lax.fori_loop(0, 4, add_half, 0)
        send(ATF + k, att_p.at[xx[e], c], att_f.at[k], x=xx[e])

    hidden(0, to_keep)

    def weight_part(e, first):
        def tile(m, carry):
            cols = pl.ds(pl.multiple_of(m * 256, 256), 256)
            part = lax.dot_general(
                ug[yy[e], :, :, cols].reshape(512, 256), ag[yy[e]], (((0,), (0,)), ((), ())),
                preferred_element_type=F32,
            ).reshape(2, 128, 1024)
            here = pl.ds(2 * m, 2)
            if first:
                acc[here] = part
            else:
                acc[here] = acc[here] + part
            return carry

        lax.fori_loop(0, 4, tile, 0)

    weight_part(0, True)
    for q in (2, 3):
        act_from_left(q, False)
    weight_part(3, False)
    for q in (0, 1):
        act_from_right(q, False)
    weight_part(1, False)
    for q in (0, 1):
        arrived(ARF + q, ag.at[yy[2], pl.ds(q * 128, 128)], y=yy[3])
    for q in (2, 3):
        arrived(ALF + q, ag.at[yy[2], pl.ds(q * 128, 128)], y=yy[1])
    weight_part(2, False)

    def grad_id(k, s, half):
        return GRS + (k * 4 + s) * 2 + half

    def grad_send(k, s, half, add):
        target = zz[4 - s] if k == 0 else zz[4 + s]
        here = pl.ds(half * 64, 64)
        came = zz[7] if k == 0 else zz[1]
        if add:
            arrived(grad_id(k, s - 1, half), gr.at[k, s - 1, here], z=came)
            gs[k, s, here, :] = (acc[target, here, :] + gr[k, s - 1, here, :].astype(F32)).astype(BF)
        else:
            gs[k, s, here, :] = acc[target, here, :].astype(BF)
        send(grad_id(k, s, half), gs.at[k, s, here], gr.at[k, s, here], z=zz[1] if k == 0 else zz[7])

    grad_send(0, 0, 0, False)
    grad_send(1, 0, 1, False)
    grad_send(0, 1, 1, False)
    grad_send(1, 1, 0, False)

    arrived(ATS, att_r.at[x], c=oc)
    for k in range(2):
        arrived(ATF + k, att_f.at[k], x=xx[3] if k == 0 else xx[1])
    got_bias.wait()

    def att_rows(i, carry):
        here = pl.ds(pl.multiple_of(i * 16, 16), 16)
        total = att_p[x, c, here, :].astype(F32) + att_r[x, here, :].astype(F32)
        total = total + att_f[0, here, :].astype(F32) + att_f[1, here, :].astype(F32)
        att_o[here, :] = total + bias_v[...].astype(F32)
        return carry

    lax.fori_loop(0, 4, att_rows, 0)
    local.append(fetch(L_ATT, att_o, att_hbm))

    grad_send(0, 1, 0, True)
    grad_send(1, 1, 1, True)
    grad_send(0, 2, 1, True)
    grad_send(1, 2, 0, True)

    def hidden_hop(k):
        slot, here = (0, top) if k == 0 else (2, bottom)
        arrived(HHS + k, hh.at[k], y=yy[3] if k == 0 else yy[1])
        start = 0 if k == 0 else 256

        def rows(i, carry):
            there = pl.ds(pl.multiple_of(i * 16, 16), 16)
            mine = pl.ds(pl.multiple_of(start + i * 16, 16), 16)
            total = hp[slot, mine, :].astype(F32) + hh[k, there, :].astype(F32)
            hp[slot, mine, :] = total.astype(BF)
            return carry

        lax.fori_loop(0, 16, rows, 0)
        send(HFS + 2 + k, hp.at[slot, here], hf.at[k, here], y=yy[1] if k == 0 else yy[3])

    hidden_hop(0)
    hidden_hop(1)
    for s, halves in ((2, (0, 1)), (3, (1, 0)), (3, (0, 1))):
        grad_send(0, s, halves[0], True)
        grad_send(1, s, halves[1], True)

    arrived(HFS, hf.at[0, bottom], y=yy[3])
    arrived(HFS + 1, hf.at[1, top], y=yy[1])

    def fold(k, start):
        def rows(i, carry):
            here = pl.ds(pl.multiple_of(start + i * 16, 16), 16)
            h0[here, :] = h0[here, :] + hf[k, here, :].astype(F32)
            return carry

        lax.fori_loop(0, 16, rows, 0)

    fold(0, 256)
    fold(1, 0)

    for half in (0, 1):
        here = pl.ds(half * 64, 64)
        for k in range(2):
            arrived(grad_id(k, 3, half), gr.at[k, 3, here], z=zz[7] if k == 0 else zz[1])
        total = acc[z, here, :] + gr[0, 3, here, :].astype(F32) + gr[1, 3, here, :].astype(F32)
        go[here, :] = total * (1.0 / 32.0)
    local.append(fetch(L_WG, go, wg_hbm))

    def finish(k, start):
        def rows(i, carry):
            here = pl.ds(pl.multiple_of(start + i * 16, 16), 16)
            h0[here, :] = (h0[here, :] + hf[k, here, :].astype(F32)) * slope_v[here, :]
            return carry

        lax.fori_loop(0, 16, rows, 0)
        part = pl.ds(start, 256)
        local.append(fetch(L_ACT + k, h0.at[part], act_hbm.at[part]))

    arrived(HFS + 2, hf.at[0, top], y=yy[3])
    finish(0, 0)
    arrived(HFS + 3, hf.at[1, bottom], y=yy[1])
    finish(1, 256)

    for copy in sent:
        copy.wait_send()
    for copy in local:
        copy.wait()


def body(qkv, segment_ids, out_weight, out_bias, upstream, pre_act, down_weight):
    hbm = pl.BlockSpec(memory_space=pl.ANY)
    vmem = pltpu.VMEM
    return pl.pallas_call(
        kernel,
        out_shape=(
            jax.ShapeDtypeStruct((64, 4096), F32),
            jax.ShapeDtypeStruct((512, 1024), F32),
            jax.ShapeDtypeStruct((128, 1024), F32),
        ),
        in_specs=[hbm] * 7,
        out_specs=(hbm,) * 3,
        scratch_shapes=[
            vmem((3, 512, 512), BF),
            vmem((1, 8, 64), jnp.int32),
            vmem((4096, 512), BF),
            vmem((1, 4096), BF),
            vmem((512, 1024), BF),
            vmem((512, 1024), F32),
            vmem((4, 8, 64, 1024), BF),
            vmem((8, 128, 1024), BF),
            vmem((4, 512, 1024), BF),
            vmem((512, 512), BF),
            vmem((4, 2, 64, 4096), BF),
            vmem((4, 64, 4096), BF),
            vmem((2, 64, 2048), BF),
            vmem((2, 64, 4096), BF),
            vmem((64, 4096), F32),
            vmem((3, 512, 1024), BF),
            vmem((2, 256, 1024), BF),
            vmem((2, 512, 1024), BF),
            vmem((512, 1024), F32),
            vmem((8, 128, 1024), F32),
            vmem((2, 4, 128, 1024), BF),
            vmem((2, 4, 128, 1024), BF),
            vmem((128, 1024), F32),
            pltpu.SemaphoreType.DMA((N_IDS,)),
            pltpu.SemaphoreType.DMA((N_IDS,)),
            pltpu.SemaphoreType.DMA((N_LOCAL,)),
        ],
        compiler_params=pltpu.CompilerParams(
            collective_id=0, has_side_effects=True, vmem_limit_bytes=63 * 1024 * 1024
        ),
        name="layer",
    )(qkv, segment_ids, out_weight, out_bias.reshape(1, -1), upstream, pre_act, down_weight)


def solution(mesh):
    finer = Mesh(mesh.devices.reshape(4, 8, 4, 2), ("y", "z", "x", "c"))
    tensor = ("x", "c")
    in_specs = (
        P(None, DP, tensor),
        P(DP, None, None),
        P(None, tensor),
        P(),
        P(DP_TENSOR, None),
        P(DP, tensor),
        P(DP, tensor),
    )
    out_specs = (P(DP_TENSOR, None), P(DP, tensor), P(DP, tensor))
    return jax.shard_map(body, mesh=finer, in_specs=in_specs, out_specs=out_specs, check_vma=False)
```

time: 342 us -> 92.3 us (0.27)
  waiting for transfers between devices: 277 us -> 0 us
  Pallas kernels: 0 us -> 85.5 us
  matrix products: 35 us -> 0 us
  between operations: 15.3 us -> 0.65 us
  starting transfers between devices: 5.46 us -> 0 us
  other arithmetic: 4.32 us -> 0 us
    reduce_scatter x2 -> x0, waiting for transfers between devices: 187 us -> none  [summed_rows(): so_far = lax.psum_scatter(so_far, axis, scatter_dimension=0, tiled=True)]
    pallas_call x0 -> x1, Pallas kernels: none -> 85.5 us  [body(): pl.pallas_call(kernel, out_shape=(jax.ShapeDtypeStruct((64, 4096), F32),...]
    all_to_all x1 -> x0, waiting for transfers between devices: 48.8 us -> none  [summed_on_arrival(): lax.all_to_all(in_blocks(shard, dim, devices), axis, 0, 0, tiled=True)]
    all_gather x2 -> x0, waiting for transfers between devices: 40.7 us -> none  [the longest x1 40.7 us: body(): whole_grad = lax.all_gather(upstream, 'tensor', axis=0, tiled=True)]
    dot_general x4 -> x0, matrix products: 31 us -> none  [the longest x1 12.8 us: body(): lax.dot_general(columns, activation, (((0,), (0,)), ((), ())), preferred_...]
    all_to_all x1 -> x0, starting transfers between devices: 5.3 us -> none  [summed_on_arrival(): lax.all_to_all(in_blocks(shard, dim, devices), axis, 0, 0, tiled=True)]
    sub x1 -> x0, matrix products: 4.02 us -> none  [attend(): exponent = jnp.where(same_image, jnp.exp(masked - row_top), 0.0)]
  transfers between devices with their start and end apart: 5 -> 0, of which waited for: 3 -> 0; matrix products, arithmetic and copies ran while one was open for 8% -> 0% of each run, Pallas kernels for 0% -> 0%
where the time goes in v1:
time: 92.3 us; the launch traced here: 92.1 us
  Pallas kernels  85.5 us (93%)
  local copies, waits for them, and re-layouts  5.92 us (6%)
    pallas_call x1, Pallas kernels, body(): pl.pallas_call(kernel, out_shape=(jax.ShapeDtypeStruct((64, 4096), F32),...  85.5 us
    unnamed x7, local copies, waits for them, and re-layouts  4.61 us

profile of v1, /device:TPU:1, one launch (start us, length us, event | category | flops | bytes accessed | tf_op | source)
XLA Modules:
  0.0 92.1 jit_solution(9875440892583207287)
XLA Ops:
  0.6 1.3 %reshape.9.bias = bf16[1,4096]{1,0:T(2,128)(2,1)} reshape(bf16[4096]{0:T(1024)(128)(2,1)} %param.10) | data formatting | bytes 16384 | tf_op jit(solution)/shard_map/reshape | solution.py:497
  1.9 85.5 %layer.1 = (f32[64,4096]{1,0:T(8,128)}, f32[512,1024]{1,0:T(8,128)}, f32[128,1024]{1,0:T(8,128)}) custom-call(bf16[3,512,512]{2,1,0:T(8,128)(2,1)} %qkv.1, s32[1,8,64]{2,1,0:T(8,128)} %seg.1, bf16[4096,512]{1,0:T(8,128)(2,1)} %out_weight.1, bf16[1,4096]{1,0:T(2,128)(2,1)} %reshape.9.bias, bf16[64,4096]{1,0:T(8,128)(2,1)} %upstream.1, ...), custom_call_target="tpu_custom_call" | custom-call | tf_op jit(solution)/shard_map/layer/pallas_call | solution.py:456
  87.5 0.0 copy-start
  87.5 2.4 %copy.13 = f32[64,4096]{1,0:T(8,128)} copy(f32[64,4096]{1,0:T(8,128)} %get-tuple-element.6) | data formatting | bytes 2097152
  89.9 0.0 copy-done
  89.9 0.0 copy-start.1
  89.9 1.3 %copy.14 = f32[512,1024]{1,0:T(8,128)} copy(f32[512,1024]{1,0:T(8,128)S(1)} %copy-done) | data formatting | bytes 4194304
  91.2 0.1 copy-done.1
  91.3 0.8 copy.15
Async XLA Ops:
  87.5 2.4 %copy-start = (f32[512,1024]{1,0:T(8,128)S(1)}, f32[512,1024]{1,0:T(8,128)}, u32[]{:S(2)}) copy-start(f32[512,1024]{1,0:T(8,128)} %get-tuple-element.7) | copy-start | bytes 6291460
  89.9 1.4 %copy-start.1 = (f32[128,1024]{1,0:T(8,128)S(1)}, f32[128,1024]{1,0:T(8,128)}, u32[]{:S(2)}) copy-start(f32[128,1024]{1,0:T(8,128)} %get-tuple-element.8) | copy-start | bytes 1572868

commit v2 on v1

v2 whole, which is shorter than its diff:
```python
import math

import jax
import jax.numpy as jnp
from jax import lax
from jax.experimental import pallas as pl
from jax.experimental.pallas import tpu as pltpu
from jax.sharding import Mesh
from jax.sharding import PartitionSpec as P

HEAD = 128
DP = ("y", "z")
DP_TENSOR = ("y", "z", "x", "c")
BF = jnp.bfloat16
F32 = jnp.float32

ROOT_HALF = 1.0 / math.sqrt(2.0)
INV_ROOT_TAU = 1.0 / math.sqrt(2.0 * math.pi)
SCALE = 1.0 / math.sqrt(HEAD)


class Ids:
    def __init__(self):
        self.n = 0

    def take(self, count=1):
        first = self.n
        self.n += count
        return first


IDS = Ids()
U1 = IDS.take(4)
U2R, U2L = IDS.take(4), IDS.take(4)
U2FR, U2FL = IDS.take(4), IDS.take(4)
U2S = IDS.take(4)
UOR, UOL = IDS.take(4), IDS.take(4)
UOFR, UOFL = IDS.take(4), IDS.take(4)
UOS = IDS.take(4)
WY = IDS.take(4)
WR, WL = IDS.take(4), IDS.take(4)
WOR, WOL = IDS.take(4), IDS.take(4)
AR, AL = IDS.take(4), IDS.take(4)
ARF, ALF = IDS.take(4), IDS.take(4)
ATS = IDS.take(4)
ATH, ATF = IDS.take(2), IDS.take(2)
HHS, HFS = IDS.take(2), IDS.take(4)
GRS = IDS.take(16)
N_IDS = IDS.n

LOCAL = Ids()
L_QKV, L_SEG, L_OW, L_PRE, L_UP, L_W, L_BIAS = (LOCAL.take() for _ in range(7))
L_UO = LOCAL.take(4)
N_LOCAL = LOCAL.n

CO = 256
CQ = 1024 - CO


def kernel(
    qkv, seg, out_weight, bias, upstream, pre_act, down_weight,
    att_o, h0, go,
    qkv_v, seg_v, ow_v, bias_v, pre_v, slope_v, ug, uo, wg, wo, ag, ctx,
    att_p, att_r, att_h, att_f,
    hp, hh, hf, acc, gs, gr,
    ssem, rsem, lsem,
):
    y, z, x, c = (lax.axis_index(name) for name in ("y", "z", "x", "c"))
    t = 2 * x + c
    yy = [lax.rem(y + d, 4) for d in range(4)]
    zz = [lax.rem(z + d, 8) for d in range(8)]
    xx = [lax.rem(x + d, 4) for d in range(4)]
    oc = 1 - c
    sent = []

    def send(k, src, dst, **where):
        copy = pltpu.make_async_remote_copy(
            src_ref=src, dst_ref=dst, send_sem=ssem.at[k], recv_sem=rsem.at[k],
            device_id=where, device_id_type=pl.DeviceIdType.MESH,
        )
        copy.start()
        sent.append(copy)

    def arrived(k, dst, **where):
        pltpu.make_async_remote_copy(
            src_ref=dst, dst_ref=dst, send_sem=ssem.at[k], recv_sem=rsem.at[k],
            device_id=where, device_id_type=pl.DeviceIdType.MESH,
        ).wait_recv()

    def fetch(k, src, dst):
        copy = pltpu.make_async_copy(src, dst, lsem.at[k])
        copy.start()
        return copy

    got_pre = fetch(L_PRE, pre_act, pre_v)
    got_w = fetch(L_W, down_weight, wg.at[z])
    got_up = fetch(L_UP, upstream.at[:, pl.ds(pl.multiple_of(y * 1024, 1024), 1024)], ug.at[y, t])
    got_seg = fetch(L_SEG, seg, seg_v)
    got_qkv = fetch(L_QKV, qkv, qkv_v)
    got_uo = [
        fetch(L_UO + e, upstream.at[:, pl.ds(pl.multiple_of(yy[e] * 1024, 1024), 1024)], uo.at[e - 1, t])
        for e in (1, 2, 3)
    ]
    got_bias = fetch(L_BIAS, bias, bias_v)
    got_ow = fetch(L_OW, out_weight, ow_v)

    barrier = pltpu.get_barrier_semaphore()
    peers = [{"y": yy[d]} for d in (1, 2, 3)] + [{"z": zz[d]} for d in (1, 7)]
    peers += [{"x": xx[d]} for d in (1, 3)] + [{"c": oc}]
    for peer in peers:
        pl.semaphore_signal(barrier, inc=1, device_id=peer, device_id_type=pl.DeviceIdType.MESH)
    pl.semaphore_wait(barrier, len(peers))

    got_w.wait()
    send(WR, wg.at[z], wg.at[z], z=zz[1])
    send(WL, wg.at[z], wg.at[z], z=zz[7])
    for d in (1, 3, 2):
        columns = pl.ds(pl.multiple_of(yy[d] * 1024, 1024), 1024)
        send(U1 + d, upstream.at[:, columns], ug.at[y, t], y=yy[d])
    for d in (1, 3, 2):
        send(WY + d, wg.at[z, :, pl.ds(CQ, CO)], wo.at[3 - d, z], y=yy[d])
    got_up.wait()
    send(U2R, ug.at[y, t], ug.at[y, t], x=xx[1])
    send(U2L, ug.at[y, t], ug.at[y, t], x=xx[3])

    got_pre.wait()

    def gelu(q):
        def rows(i, carry):
            here = pl.ds(pl.multiple_of(q * 128 + i * 16, 16), 16)
            v = pre_v[here, :].astype(F32)
            tail = 1.0 + lax.erf(v * ROOT_HALF)
            ag[y, here, :] = (0.5 * v * tail).astype(BF)
            slope_v[here, :] = 0.5 * tail + v * jnp.exp(-0.5 * v * v) * INV_ROOT_TAU
            return carry

        lax.fori_loop(0, 8, rows, 0)

    def act_own(q):
        part = pl.ds(q * 128, 128)
        send(AR + q, ag.at[y, part], ag.at[y, part], y=yy[1])
        send(AL + q, ag.at[y, part], ag.at[y, part], y=yy[3])

    def act_hop(q):
        part = pl.ds(q * 128, 128)
        low_slot, high_slot = ag.at[yy[3], part], ag.at[yy[1], part]
        arrived(AR + q, low_slot, y=yy[3])
        if q % 2 == 0:
            send(ARF + q, low_slot, low_slot, y=yy[1])
        arrived(AL + q, high_slot, y=yy[1])
        if q % 2 == 1:
            send(ALF + q, high_slot, high_slot, y=yy[3])

    def act_far():
        for q in range(4):
            slot = ag.at[yy[2], pl.ds(q * 128, 128)]
            if q % 2 == 0:
                arrived(ARF + q, slot, y=yy[3])
            else:
                arrived(ALF + q, slot, y=yy[1])

    def own_upstream(e):
        slot = ug.at[yy[e], t]
        arrived(U1 + (4 - e), slot, y=yy[e])
        send(U2R + e, slot, slot, x=xx[1])
        send(U2L + e, slot, slot, x=xx[3])

    t_left, t_right, t_far = 2 * xx[3] + c, 2 * xx[1] + c, 2 * xx[2] + c

    def upstream_hop(e):
        left, right = ug.at[yy[e], t_left], ug.at[yy[e], t_right]
        arrived(U2R + e, left, x=xx[3])
        if e in (0, 1):
            send(U2FR + e, left, left, x=xx[1])
        arrived(U2L + e, right, x=xx[1])
        if e in (2, 3):
            send(U2FL + e, right, right, x=xx[3])

    def upstream_far():
        for e in (0, 1):
            arrived(U2FR + e, ug.at[yy[e], t_far], x=xx[3])
        for e in (3, 2):
            arrived(U2FL + e, ug.at[yy[e], t_far], x=xx[1])

    def others_own(e):
        got_uo[e - 1].wait()
        slot = uo.at[e - 1, t]
        send(UOR + e, slot, slot, x=xx[1])
        send(UOL + e, slot, slot, x=xx[3])

    first, last = pl.ds(0, 32), pl.ds(32, 32)

    def others_hop(e):
        left, right = uo.at[e - 1, t_left], uo.at[e - 1, t_right]
        arrived(UOR + e, left, x=xx[3])
        if e == 1:
            send(UOFR + e, left, left, x=xx[1])
        if e == 2:
            send(UOFR + e, left.at[first], left.at[first], x=xx[1])
        arrived(UOL + e, right, x=xx[1])
        if e == 3:
            send(UOFL + e, right, right, x=xx[3])
        if e == 2:
            send(UOFL + e, right.at[last], right.at[last], x=xx[3])

    def others_far():
        arrived(UOFR + 1, uo.at[0, t_far], x=xx[3])
        arrived(UOFR + 2, uo.at[1, t_far].at[first], x=xx[3])
        arrived(UOFL + 3, uo.at[2, t_far], x=xx[1])
        arrived(UOFL + 2, uo.at[1, t_far].at[last], x=xx[1])

    low, high = pl.ds(0, 64), pl.ds(64, 64)

    def weight_hop(s):
        from_left, from_right = zz[8 - s], zz[s]
        arrived(WR + s - 1, wg.at[from_left], z=zz[7])
        left, right = wg.at[from_left], wg.at[from_right]
        if s == 3:
            left, right = wg.at[from_left, low], wg.at[from_right, high]
        send(WR + s, left, left, z=zz[1])
        arrived(WL + s - 1, wg.at[from_right], z=zz[1])
        send(WL + s, right, right, z=zz[7])

    def weight_far():
        arrived(WR + 3, wg.at[zz[4], low], z=zz[7])
        arrived(WL + 3, wg.at[zz[4], high], z=zz[1])

    def side_own():
        for e in (1, 3, 2):
            arrived(WY + 4 - e, wo.at[e - 1, z], y=yy[e])
        send(WOR, wo.at[:, z], wo.at[:, z], z=zz[1])
        send(WOL, wo.at[:, z], wo.at[:, z], z=zz[7])

    def side_hop(s):
        from_left, from_right = zz[8 - s], zz[s]
        arrived(WOR + s - 1, wo.at[:, from_left], z=zz[7])
        left, right = wo.at[:, from_left], wo.at[:, from_right]
        if s == 3:
            left, right = wo.at[:, from_left, low], wo.at[:, from_right, high]
        send(WOR + s, left, left, z=zz[1])
        arrived(WOL + s - 1, wo.at[:, from_right], z=zz[1])
        send(WOL + s, right, right, z=zz[7])

    def side_far():
        arrived(WOR + 3, wo.at[:, zz[4], low], z=zz[7])
        arrived(WOL + 3, wo.at[:, zz[4], high], z=zz[1])

    def attend(pair):
        labels = seg_v[0].astype(F32)
        row_i = lax.broadcasted_iota(jnp.int32, (128, 1), 0)
        col_i = lax.broadcasted_iota(jnp.int32, (1, 128), 1)
        starts = [
            (64.0 - jnp.sum(labels[2 * pair + p : 2 * pair + p + 1, :], axis=1, keepdims=True)).astype(jnp.int32)
            for p in range(2)
        ]

        def image(i):
            second_pack = i >= 64
            place = jnp.where(second_pack, i - 64, i)
            bound = jnp.where(second_pack, starts[1], starts[0])
            return jnp.where(second_pack, 2, 0) + jnp.where(place >= bound, 1, 0)

        same = image(row_i) == image(col_i)
        rows = pl.ds(pair * 128, 128)
        for h in range(4):
            cols = pl.ds(h * 128, 128)
            s = lax.dot_general(
                qkv_v[0, rows, cols], qkv_v[1, rows, cols], (((1,), (1,)), ((), ())),
                preferred_element_type=F32,
            ) * SCALE
            s = jnp.where(same, s, -1e30)
            e = jnp.where(same, jnp.exp(s - jnp.max(s, axis=1, keepdims=True)), 0.0)
            w = (e / jnp.sum(e, axis=1, keepdims=True)).astype(BF)
            ctx[rows, cols] = jnp.dot(w, qkv_v[2, rows, cols], preferred_element_type=F32).astype(BF)

    def project(n, carry):
        cols = pl.ds(pl.multiple_of(n * 512, 512), 512)
        part = lax.dot_general(
            ctx[...], ow_v[cols, :], (((1,), (1,)), ((), ())), preferred_element_type=F32
        )
        att_p[:, :, :, cols] = part.astype(BF).reshape(4, 2, 64, 512)
        return carry

    def chip_sum(e):
        arrived(ATS + e, att_r.at[xx[e]], c=oc)

        def rows(i, carry):
            here = pl.ds(pl.multiple_of(i * 16, 16), 16)
            both = att_p[xx[e], c, here, :].astype(F32) + att_r[xx[e], here, :].astype(F32)
            att_p[xx[e], c, here, :] = both.astype(BF)
            return carry

        lax.fori_loop(0, 4, rows, 0)

    def att_first():
        chip_sum(2)
        for k, cols in enumerate((pl.ds(0, 2048), pl.ds(2048, 2048))):
            send(ATH + k, att_p.at[xx[2], c, :, cols], att_h.at[k], x=xx[1] if k == 0 else xx[3])
        for e in (1, 3):
            chip_sum(e)

    def att_second():
        for k, e, lo in ((0, 1, 0), (1, 3, 2048)):
            arrived(ATH + k, att_h.at[k], x=xx[3] if k == 0 else xx[1])

            def add_half(i, carry, k=k, e=e, lo=lo):
                here = pl.ds(pl.multiple_of(i * 16, 16), 16)
                cols = pl.ds(lo, 2048)
                total = att_p[xx[e], c, here, cols].astype(F32) + att_h[k, here, :].astype(F32)
                att_p[xx[e], c, here, cols] = total.astype(BF)
                return carry

            lax.fori_loop(0, 4, add_half, 0)
            send(ATF + k, att_p.at[xx[e], c], att_f.at[k], x=xx[e])

    def att_last():
        arrived(ATS, att_r.at[x], c=oc)
        for k in range(2):
            arrived(ATF + k, att_f.at[k], x=xx[3] if k == 0 else xx[1])
        got_bias.wait()
        row = bias_v[...].astype(F32).reshape(1, 4096)

        def att_rows(i, carry):
            here = pl.ds(pl.multiple_of(i * 16, 16), 16)
            total = att_p[x, c, here, :].astype(F32) + att_r[x, here, :].astype(F32)
            total = total + att_f[0, here, :].astype(F32) + att_f[1, here, :].astype(F32)
            att_o[here, :] = total + row
            return carry

        lax.fori_loop(0, 4, att_rows, 0)

    def hidden(d, store):
        def tile(n, carry):
            cols = pl.ds(pl.multiple_of(n * 256, 256), 256)
            store(
                cols,
                jnp.dot(
                    ug[yy[d]].reshape(512, 1024), wg[:, :, cols].reshape(1024, 256),
                    preferred_element_type=F32,
                ),
            )
            return carry

        lax.fori_loop(0, CQ // 256, tile, 0)

    def to_send(d):
        def store(cols, value):
            hp[d - 1, :, cols] = value.astype(BF)

        return store

    def to_keep(cols, value):
        h0[:, cols] = value

    side_cols = pl.ds(CQ, CO)

    def hidden_side():
        def rows(i, carry):
            total = jnp.dot(
                ug[y, pl.ds(2 * i, 2)].reshape(128, 1024), wg[:, :, side_cols].reshape(1024, CO),
                preferred_element_type=F32,
            )
            for e in range(3):
                total = total + jnp.dot(
                    uo[e, pl.ds(2 * i, 2)].reshape(128, 1024), wo[e].reshape(1024, CO),
                    preferred_element_type=F32,
                )
            here = pl.ds(pl.multiple_of(i * 128, 128), 128)
            h0[here, side_cols] = total * slope_v[here, side_cols]
            return carry

        lax.fori_loop(0, 4, rows, 0)

    def weight_part(e, start):
        def tile(m, carry):
            cols = pl.ds(pl.multiple_of(m * 256, 256), 256)
            part = lax.dot_general(
                ug[yy[e], :, :, cols].reshape(512, 256), ag[yy[e]], (((0,), (0,)), ((), ())),
                preferred_element_type=F32,
            ).reshape(2, 128, 1024)
            here = pl.ds(2 * m, 2)
            if start:
                acc[here] = part
            else:
                acc[here] = acc[here] + part
            return carry

        lax.fori_loop(0, 4, tile, 0)

    def weight_tile(e, i):
        m = lax.rem((z + 4) // 2 + i, 4)
        cols = pl.ds(pl.multiple_of(m * 256, 256), 256)
        part = lax.dot_general(
            ug[yy[e], :, :, cols].reshape(512, 256), ag[yy[e]], (((0,), (0,)), ((), ())),
            preferred_element_type=F32,
        ).reshape(2, 128, 1024)
        here = pl.ds(2 * m, 2)
        acc[here] = acc[here] + part

    def grad_id(k, s, half):
        return GRS + (k * 4 + s) * 2 + half

    def grad_send(k, s, half, add):
        target = zz[4 - s] if k == 0 else zz[4 + s]
        here = pl.ds(half * 64, 64)
        came = zz[7] if k == 0 else zz[1]
        if add:
            arrived(grad_id(k, s - 1, half), gr.at[k, s - 1, here], z=came)
            gs[k, s, here, :] = (acc[target, here, :] + gr[k, s - 1, here, :].astype(F32)).astype(BF)
        else:
            gs[k, s, here, :] = acc[target, here, :].astype(BF)
        send(grad_id(k, s, half), gs.at[k, s, here], gr.at[k, s, here], z=zz[1] if k == 0 else zz[7])

    top, bottom = pl.ds(0, 256), pl.ds(256, 256)

    def hidden_hop(k):
        slot, here = (0, top) if k == 0 else (2, bottom)
        arrived(HHS + k, hh.at[k], y=yy[3] if k == 0 else yy[1])
        start = 0 if k == 0 else 256

        def rows(i, carry):
            there = pl.ds(pl.multiple_of(i * 16, 16), 16)
            mine = pl.ds(pl.multiple_of(start + i * 16, 16), 16)
            total = hp[slot, mine, :].astype(F32) + hh[k, there, :].astype(F32)
            hp[slot, mine, :] = total.astype(BF)
            return carry

        lax.fori_loop(0, 16, rows, 0)
        send(HFS + 2 + k, hp.at[slot, here], hf.at[k, here], y=yy[1] if k == 0 else yy[3])

    main_cols = pl.ds(0, CQ)

    def fold(k, start):
        def rows(i, carry):
            here = pl.ds(pl.multiple_of(start + i * 16, 16), 16)
            h0[here, main_cols] = h0[here, main_cols] + hf[k, here, :].astype(F32)
            return carry

        lax.fori_loop(0, 16, rows, 0)

    def finish(k, start):
        def rows(i, carry):
            here = pl.ds(pl.multiple_of(start + i * 16, 16), 16)
            total = h0[here, main_cols] + hf[k, here, :].astype(F32)
            h0[here, main_cols] = total * slope_v[here, main_cols]
            return carry

        lax.fori_loop(0, 16, rows, 0)

    gelu(0)
    act_own(0)
    gelu(1)
    gelu(2)
    gelu(3)
    got_seg.wait()
    got_qkv.wait()
    for pair in range(4):
        attend(pair)
    weight_hop(1)
    act_own(1)
    got_ow.wait()
    lax.fori_loop(0, 3, project, 0)
    side_own()
    for e in (3, 1, 2):
        own_upstream(e)
    send(U2S, ug.at[:, t], ug.at[:, t], c=oc)
    lax.fori_loop(3, 8, project, 0)
    for e in (2, 1, 3, 0):
        send(ATS + e, att_p.at[xx[e], oc], att_r.at[xx[e]], c=oc)
    act_hop(0)
    act_own(2)
    weight_hop(2)
    upstream_hop(0)
    upstream_hop(3)
    side_hop(1)
    act_hop(1)
    act_own(3)
    upstream_hop(1)
    upstream_hop(2)
    send(U2S + 1, ug.at[:, t_left], ug.at[:, t_left], c=oc)
    send(U2S + 2, ug.at[:, t_right], ug.at[:, t_right], c=oc)
    for e in (1, 3, 2):
        others_own(e)
    send(UOS, uo.at[:, t], uo.at[:, t], c=oc)
    weight_hop(3)
    side_hop(2)
    act_hop(2)
    upstream_far()
    send(U2S + 3, ug.at[:, t_far], ug.at[:, t_far], c=oc)
    att_first()
    for k, dx in ((0, 0), (1, 3), (2, 1), (3, 2)):
        arrived(U2S + k, ug.at[:, 2 * xx[dx] + oc], c=oc)
    weight_part(0, True)
    weight_far()
    hidden(2, to_send(2))
    side_hop(3)
    act_hop(3)
    send(HHS, hp.at[1, top], hh.at[0], y=yy[1])
    send(HHS + 1, hp.at[1, bottom], hh.at[1], y=yy[3])
    for e in (1, 3, 2):
        others_hop(e)
    send(UOS + 1, uo.at[:, t_left], uo.at[:, t_left], c=oc)
    send(UOS + 2, uo.at[:, t_right], uo.at[:, t_right], c=oc)
    weight_part(3, False)
    weight_part(1, False)
    att_second()
    act_far()
    weight_tile(2, 0)
    grad_send(0, 0, 0, False)
    grad_send(1, 0, 1, False)
    lax.fori_loop(1, 4, lambda i, carry: weight_tile(2, i), None)
    grad_send(0, 1, 1, False)
    grad_send(1, 1, 0, False)
    hidden(1, to_send(1))
    send(HFS, hp.at[0, bottom], hf.at[0, bottom], y=yy[1])
    hidden(3, to_send(3))
    send(HFS + 1, hp.at[2, top], hf.at[1, top], y=yy[3])
    others_far()
    send(UOS + 3, uo.at[:, t_far], uo.at[:, t_far], c=oc)
    side_far()
    grad_send(0, 1, 0, True)
    grad_send(1, 1, 1, True)
    grad_send(0, 2, 1, True)
    grad_send(1, 2, 0, True)
    hidden_hop(0)
    hidden_hop(1)
    hidden(0, to_keep)
    grad_send(0, 2, 0, True)
    grad_send(1, 2, 1, True)
    grad_send(0, 3, 1, True)
    grad_send(1, 3, 0, True)
    for k, dx in ((0, 0), (1, 3), (2, 1), (3, 2)):
        arrived(UOS + k, uo.at[:, 2 * xx[dx] + oc], c=oc)
    hidden_side()
    grad_send(0, 3, 0, True)
    grad_send(1, 3, 1, True)
    att_last()

    arrived(HFS, hf.at[0, bottom], y=yy[3])
    arrived(HFS + 1, hf.at[1, top], y=yy[1])
    fold(0, 256)
    fold(1, 0)

    def grad_last(half):
        here = pl.ds(half * 64, 64)
        for k in range(2):
            arrived(grad_id(k, 3, half), gr.at[k, 3, here], z=zz[7] if k == 0 else zz[1])
        total = acc[z, here, :] + gr[0, 3, here, :].astype(F32) + gr[1, 3, here, :].astype(F32)
        go[here, :] = total * (1.0 / 32.0)

    grad_last(0)
    grad_last(1)
    arrived(HFS + 2, hf.at[0, top], y=yy[3])
    finish(0, 0)
    arrived(HFS + 3, hf.at[1, bottom], y=yy[1])
    finish(1, 256)

    for copy in sent:
        copy.wait_send()


def body(*args):
    hbm = pl.BlockSpec(memory_space=pltpu.HBM)
    vmem = pltpu.VMEM
    return pl.pallas_call(
        kernel,
        out_shape=(
            jax.ShapeDtypeStruct((64, 4096), F32),
            jax.ShapeDtypeStruct((512, 1024), F32),
            jax.ShapeDtypeStruct((128, 1024), F32),
        ),
        in_specs=[hbm] * 7,
        out_specs=(pl.BlockSpec(memory_space=pltpu.VMEM),) * 3,
        scratch_shapes=[
            vmem((3, 512, 512), BF),
            vmem((1, 8, 64), jnp.int32),
            vmem((4096, 512), BF),
            vmem((4096,), BF),
            vmem((512, 1024), BF),
            vmem((512, 1024), F32),
            vmem((4, 8, 64, 1024), BF),
            vmem((3, 8, 64, 1024), BF),
            vmem((8, 128, 1024), BF),
            vmem((3, 8, 128, CO), BF),
            vmem((4, 512, 1024), BF),
            vmem((512, 512), BF),
            vmem((4, 2, 64, 4096), BF),
            vmem((4, 64, 4096), BF),
            vmem((2, 64, 2048), BF),
            vmem((2, 64, 4096), BF),
            vmem((3, 512, CQ), BF),
            vmem((2, 256, CQ), BF),
            vmem((2, 512, CQ), BF),
            vmem((8, 128, 1024), F32),
            vmem((2, 4, 128, 1024), BF),
            vmem((2, 4, 128, 1024), BF),
            pltpu.SemaphoreType.DMA((N_IDS,)),
            pltpu.SemaphoreType.DMA((N_IDS,)),
            pltpu.SemaphoreType.DMA((N_LOCAL,)),
        ],
        compiler_params=pltpu.CompilerParams(
            collective_id=0, has_side_effects=True, vmem_limit_bytes=50 * 1024 * 1024
        ),
        name="layer",
    )(*(pltpu.with_memory_space_constraint(a, pltpu.HBM) for a in args))


def solution(mesh):
    finer = Mesh(mesh.devices.reshape(4, 8, 4, 2), ("y", "z", "x", "c"))
    tensor = ("x", "c")
    in_specs = (
        P(None, DP, tensor),
        P(DP, None, None),
        P(None, tensor),
        P(),
        P(DP_TENSOR, None),
        P(DP, tensor),
        P(DP, tensor),
    )
    out_specs = (P(DP_TENSOR, None), P(DP, tensor), P(DP, tensor))
    return jax.shard_map(body, mesh=finer, in_specs=in_specs, out_specs=out_specs, check_vma=False)
```

time: 92.3 us -> 85.1 us (0.922)
  Pallas kernels: 85.5 us -> 80.3 us
  local copies, waits for them, and re-layouts: 5.92 us -> 3.08 us
    pallas_call x1, Pallas kernels: 85.5 us -> 80.3 us  [body(): pl.pallas_call(kernel, out_shape=(jax.ShapeDtypeStruct((64, 4096), F32),...]
    unnamed x7 -> x3, local copies, waits for them, and re-layouts: 4.61 us -> 3.08 us
    reshape x1 -> x0, local copies, waits for them, and re-layouts: 1.31 us -> none  [body(): out_bias.reshape(1, -1)]
where the time goes in v2:
time: 85.1 us; the launch traced here: 84 us
  Pallas kernels  80.3 us (94%)
  local copies, waits for them, and re-layouts  3.08 us (4%)
    pallas_call x1, Pallas kernels, body(): pl.pallas_call(kernel, out_shape=(jax.ShapeDtypeStruct((64, 4096), F32),...  80.3 us
    unnamed x3, local copies, waits for them, and re-layouts  3.08 us

profile of v2, /device:TPU:1, one launch (start us, length us, event | category | flops | bytes accessed | tf_op | source)
XLA Modules:
  0.0 84.0 jit_solution(15892912538359880128)
XLA Ops:
  0.6 80.3 %layer.1 = (f32[64,4096]{1,0:T(8,128)S(1)}, f32[512,1024]{1,0:T(8,128)S(1)}, f32[128,1024]{1,0:T(8,128)S(1)}) custom-call(bf16[3,512,512]{2,1,0:T(8,128)(2,1)} %qkv.1, s32[1,8,64]{2,1,0:T(8,128)} %seg.1, bf16[4096,512]{1,0:T(8,128)(2,1)} %out_weight.1, bf16[4096]{0:T(1024)(128)(2,1)} %bias.1, bf16[64,4096]{1,0:T(8,128)(2,1)} %upstream.1, ...), custom_call_target="tpu_custom_call" | custom-call | tf_op jit(solution)/shard_map/layer/pallas_call | solution.py:565
  80.9 1.0 %copy.13 = f32[64,4096]{1,0:T(8,128)} copy(f32[64,4096]{1,0:T(8,128)S(1)} %get-tuple-element.6) | data formatting | bytes 2097152
  81.9 1.3 %copy.14 = f32[512,1024]{1,0:T(8,128)} copy(f32[512,1024]{1,0:T(8,128)S(1)} %get-tuple-element.7) | data formatting | bytes 4194304
  83.2 0.8 copy.15

commit v3 on v2

--- a/solution.py
+++ b/solution.py
@@ -31,12 +31,12 @@
 
 IDS = Ids()
 U1 = IDS.take(4)
-U2R, U2L = IDS.take(4), IDS.take(4)
-U2FR, U2FL = IDS.take(4), IDS.take(4)
-U2S = IDS.take(4)
-UOR, UOL = IDS.take(4), IDS.take(4)
-UOFR, UOFL = IDS.take(4), IDS.take(4)
-UOS = IDS.take(4)
+UPR, UPL = IDS.take(4), IDS.take(4)
+UPFR, UPFL = IDS.take(4), IDS.take(4)
+UPS = IDS.take(4)
+URR, URL = IDS.take(4), IDS.take(4)
+URFR, URFL = IDS.take(4), IDS.take(4)
+URS = IDS.take(4)
 WY = IDS.take(4)
 WR, WL = IDS.take(4), IDS.take(4)
 WOR, WOL = IDS.take(4), IDS.take(4)
@@ -46,23 +46,29 @@
 ATH, ATF = IDS.take(2), IDS.take(2)
 HHS, HFS = IDS.take(2), IDS.take(4)
 GRS = IDS.take(16)
-N_IDS = IDS.n
+GOS = IDS.take(16)
+GYS = IDS.take(4)
+N_IDS = 109
+N_SEND = 40
 
 LOCAL = Ids()
-L_QKV, L_SEG, L_OW, L_PRE, L_UP, L_W, L_BIAS = (LOCAL.take() for _ in range(7))
-L_UO = LOCAL.take(4)
+L_QKV, L_SEG, L_OW, L_PRE, L_W, L_BIAS = (LOCAL.take() for _ in range(6))
+L_UP = LOCAL.take(4)
 N_LOCAL = LOCAL.n
 
 CO = 256
 CQ = 1024 - CO
+CW = 128
+CA = 1024 - CW
+TOP = 288
 
 
 def kernel(
     qkv, seg, out_weight, bias, upstream, pre_act, down_weight,
     att_o, h0, go,
-    qkv_v, seg_v, ow_v, bias_v, pre_v, slope_v, ug, uo, wg, wo, ag, ctx,
+    qkv_v, seg_v, ow_v, bias_v, pre_v, slope_v, up, ur, wg, wo, ag, ctx,
     att_p, att_r, att_h, att_f,
-    hp, hh, hf, acc, gs, gr,
+    hp, hh, hf, acc, gs, gr, gp, gq, gy,
     ssem, rsem, lsem,
 ):
     y, z, x, c = (lax.axis_index(name) for name in ("y", "z", "x", "c"))
@@ -72,10 +78,17 @@
     xx = [lax.rem(x + d, 4) for d in range(4)]
     oc = 1 - c
     sent = []
+    place = {}
+
+    def spot(k):
+        return place.setdefault(k, len(place))
 
     def send(k, src, dst, **where):
+        n = len(sent)
+        if n >= N_SEND:
+            sent[n - N_SEND].wait_send()
         copy = pltpu.make_async_remote_copy(
-            src_ref=src, dst_ref=dst, send_sem=ssem.at[k], recv_sem=rsem.at[k],
+            src_ref=src, dst_ref=dst, send_sem=ssem.at[n % N_SEND], recv_sem=rsem.at[spot(k)],
             device_id=where, device_id_type=pl.DeviceIdType.MESH,
         )
         copy.start()
@@ -83,7 +96,7 @@
 
     def arrived(k, dst, **where):
         pltpu.make_async_remote_copy(
-            src_ref=dst, dst_ref=dst, send_sem=ssem.at[k], recv_sem=rsem.at[k],
+            src_ref=dst, dst_ref=dst, send_sem=ssem.at[0], recv_sem=rsem.at[spot(k)],
             device_id=where, device_id_type=pl.DeviceIdType.MESH,
         ).wait_recv()
 
@@ -94,13 +107,12 @@
 
     got_pre = fetch(L_PRE, pre_act, pre_v)
     got_w = fetch(L_W, down_weight, wg.at[z])
-    got_up = fetch(L_UP, upstream.at[:, pl.ds(pl.multiple_of(y * 1024, 1024), 1024)], ug.at[y, t])
+    got_up = [
+        fetch(L_UP + e, upstream.at[:, pl.ds(pl.multiple_of(yy[e] * 1024, 1024), 1024)], up.at[e, t])
+        for e in range(4)
+    ]
     got_seg = fetch(L_SEG, seg, seg_v)
     got_qkv = fetch(L_QKV, qkv, qkv_v)
-    got_uo = [
-        fetch(L_UO + e, upstream.at[:, pl.ds(pl.multiple_of(yy[e] * 1024, 1024), 1024)], uo.at[e - 1, t])
-        for e in (1, 2, 3)
-    ]
     got_bias = fetch(L_BIAS, bias, bias_v)
     got_ow = fetch(L_OW, out_weight, ow_v)
 
@@ -115,14 +127,21 @@
     send(WR, wg.at[z], wg.at[z], z=zz[1])
     send(WL, wg.at[z], wg.at[z], z=zz[7])
     for d in (1, 3, 2):
-        columns = pl.ds(pl.multiple_of(yy[d] * 1024, 1024), 1024)
-        send(U1 + d, upstream.at[:, columns], ug.at[y, t], y=yy[d])
-    for d in (1, 3, 2):
         send(WY + d, wg.at[z, :, pl.ds(CQ, CO)], wo.at[3 - d, z], y=yy[d])
-    got_up.wait()
-    send(U2R, ug.at[y, t], ug.at[y, t], x=xx[1])
-    send(U2L, ug.at[y, t], ug.at[y, t], x=xx[3])
-
+
+    for copy in got_up:
+        copy.wait()
+
+    def own_first(e):
+        send(UPR + e, up.at[e, t], up.at[e, t], x=xx[1])
+        send(UPL + e, up.at[e, t], up.at[e, t], x=xx[3])
+
+    def to_others():
+        for d in (1, 3, 2):
+            send(U1 + d, up.at[d, t], ur.at[3 - d, t], y=yy[d])
+
+    own_first(0)
+    own_first(1)
     got_pre.wait()
 
     def gelu(q):
@@ -136,14 +155,16 @@
 
         lax.fori_loop(0, 8, rows, 0)
 
+    act_cols = pl.ds(0, CA)
+
     def act_own(q):
-        part = pl.ds(q * 128, 128)
-        send(AR + q, ag.at[y, part], ag.at[y, part], y=yy[1])
-        send(AL + q, ag.at[y, part], ag.at[y, part], y=yy[3])
+        mine = ag.at[y, pl.ds(q * 128, 128), act_cols]
+        send(AR + q, mine, mine, y=yy[1])
+        send(AL + q, mine, mine, y=yy[3])
 
     def act_hop(q):
         part = pl.ds(q * 128, 128)
-        low_slot, high_slot = ag.at[yy[3], part], ag.at[yy[1], part]
+        low_slot, high_slot = ag.at[yy[3], part, act_cols], ag.at[yy[1], part, act_cols]
         arrived(AR + q, low_slot, y=yy[3])
         if q % 2 == 0:
             send(ARF + q, low_slot, low_slot, y=yy[1])
@@ -153,61 +174,71 @@
 
     def act_far():
         for q in range(4):
-            slot = ag.at[yy[2], pl.ds(q * 128, 128)]
+            slot = ag.at[yy[2], pl.ds(q * 128, 128), act_cols]
             if q % 2 == 0:
                 arrived(ARF + q, slot, y=yy[3])
             else:
                 arrived(ALF + q, slot, y=yy[1])
 
-    def own_upstream(e):
-        slot = ug.at[yy[e], t]
+    t_left, t_right, t_far = 2 * xx[3] + c, 2 * xx[1] + c, 2 * xx[2] + c
+    first, last = pl.ds(0, 32), pl.ds(32, 32)
+
+    def own_hop(e):
+        left, right = up.at[e, t_left], up.at[e, t_right]
+        arrived(UPR + e, left, x=xx[3])
+        if e in (0, 1):
+            send(UPFR + e, left, left, x=xx[1])
+        arrived(UPL + e, right, x=xx[1])
+        if e in (2, 3):
+            send(UPFL + e, right, right, x=xx[3])
+
+    def own_far():
+        for e in (0, 1):
+            arrived(UPFR + e, up.at[e, t_far], x=xx[3])
+        for e in (2, 3):
+            arrived(UPFL + e, up.at[e, t_far], x=xx[1])
+
+    def other_first(e):
+        slot = ur.at[e - 1, t]
         arrived(U1 + (4 - e), slot, y=yy[e])
-        send(U2R + e, slot, slot, x=xx[1])
-        send(U2L + e, slot, slot, x=xx[3])
-
-    t_left, t_right, t_far = 2 * xx[3] + c, 2 * xx[1] + c, 2 * xx[2] + c
-
-    def upstream_hop(e):
-        left, right = ug.at[yy[e], t_left], ug.at[yy[e], t_right]
-        arrived(U2R + e, left, x=xx[3])
-        if e in (0, 1):
-            send(U2FR + e, left, left, x=xx[1])
-        arrived(U2L + e, right, x=xx[1])
-        if e in (2, 3):
-            send(U2FL + e, right, right, x=xx[3])
-
-    def upstream_far():
-        for e in (0, 1):
-            arrived(U2FR + e, ug.at[yy[e], t_far], x=xx[3])
-        for e in (3, 2):
-            arrived(U2FL + e, ug.at[yy[e], t_far], x=xx[1])
-
-    def others_own(e):
-        got_uo[e - 1].wait()
-        slot = uo.at[e - 1, t]
-        send(UOR + e, slot, slot, x=xx[1])
-        send(UOL + e, slot, slot, x=xx[3])
-
-    first, last = pl.ds(0, 32), pl.ds(32, 32)
-
-    def others_hop(e):
-        left, right = uo.at[e - 1, t_left], uo.at[e - 1, t_right]
-        arrived(UOR + e, left, x=xx[3])
+        send(URR + e, slot, slot, x=xx[1])
+        send(URL + e, slot, slot, x=xx[3])
+
+    def other_hop(e):
+        left, right = ur.at[e - 1, t_left], ur.at[e - 1, t_right]
+        arrived(URR + e, left, x=xx[3])
         if e == 1:
-            send(UOFR + e, left, left, x=xx[1])
+            send(URFR + e, left, left, x=xx[1])
         if e == 2:
-            send(UOFR + e, left.at[first], left.at[first], x=xx[1])
-        arrived(UOL + e, right, x=xx[1])
+            send(URFR + e, left.at[first], left.at[first], x=xx[1])
+        arrived(URL + e, right, x=xx[1])
         if e == 3:
-            send(UOFL + e, right, right, x=xx[3])
+            send(URFL + e, right, right, x=xx[3])
         if e == 2:
-            send(UOFL + e, right.at[last], right.at[last], x=xx[3])
-
-    def others_far():
-        arrived(UOFR + 1, uo.at[0, t_far], x=xx[3])
-        arrived(UOFR + 2, uo.at[1, t_far].at[first], x=xx[3])
-        arrived(UOFL + 3, uo.at[2, t_far], x=xx[1])
-        arrived(UOFL + 2, uo.at[1, t_far].at[last], x=xx[1])
+            send(URFL + e, right.at[last], right.at[last], x=xx[3])
+
+    def other_far():
+        arrived(URFR + 1, ur.at[0, t_far], x=xx[3])
+        arrived(URFR + 2, ur.at[1, t_far].at[first], x=xx[3])
+        arrived(URFL + 3, ur.at[2, t_far], x=xx[1])
+        arrived(URFL + 2, ur.at[1, t_far].at[last], x=xx[1])
+
+    def own_twin(k, slot):
+        send(UPS + k, up.at[:, slot], up.at[:, slot], c=oc)
+
+    def other_twin(k, slot):
+        send(URS + k, ur.at[:, slot], ur.at[:, slot], c=oc)
+
+    def own_all():
+        for k, dx in ((0, 0), (1, 3), (2, 1), (3, 2)):
+            arrived(UPS + k, up.at[:, 2 * xx[dx] + oc], c=oc)
+
+    def other_all():
+        for k, dx in ((0, 0), (1, 3), (2, 1), (3, 2)):
+            arrived(URS + k, ur.at[:, 2 * xx[dx] + oc], c=oc)
+
+    def tokens(e):
+        return up.at[0] if e == 0 else ur.at[e - 1]
 
     low, high = pl.ds(0, 64), pl.ds(64, 64)
 
@@ -335,7 +366,7 @@
             store(
                 cols,
                 jnp.dot(
-                    ug[yy[d]].reshape(512, 1024), wg[:, :, cols].reshape(1024, 256),
+                    tokens(d)[...].reshape(512, 1024), wg[:, :, cols].reshape(1024, 256),
                     preferred_element_type=F32,
                 ),
             )
@@ -357,12 +388,12 @@
     def hidden_side():
         def rows(i, carry):
             total = jnp.dot(
-                ug[y, pl.ds(2 * i, 2)].reshape(128, 1024), wg[:, :, side_cols].reshape(1024, CO),
+                up[0, pl.ds(2 * i, 2)].reshape(128, 1024), wg[:, :, side_cols].reshape(1024, CO),
                 preferred_element_type=F32,
             )
             for e in range(3):
                 total = total + jnp.dot(
-                    uo[e, pl.ds(2 * i, 2)].reshape(128, 1024), wo[e].reshape(1024, CO),
+                    up[e + 1, pl.ds(2 * i, 2)].reshape(128, 1024), wo[e].reshape(1024, CO),
                     preferred_element_type=F32,
                 )
             here = pl.ds(pl.multiple_of(i * 128, 128), 128)
@@ -375,9 +406,9 @@
         def tile(m, carry):
             cols = pl.ds(pl.multiple_of(m * 256, 256), 256)
             part = lax.dot_general(
-                ug[yy[e], :, :, cols].reshape(512, 256), ag[yy[e]], (((0,), (0,)), ((), ())),
+                tokens(e)[:, :, cols].reshape(512, 256), ag[yy[e], :, act_cols], (((0,), (0,)), ((), ())),
                 preferred_element_type=F32,
-            ).reshape(2, 128, 1024)
+            ).reshape(2, 128, CA)
             here = pl.ds(2 * m, 2)
             if start:
                 acc[here] = part
@@ -391,9 +422,9 @@
         m = lax.rem((z + 4) // 2 + i, 4)
         cols = pl.ds(pl.multiple_of(m * 256, 256), 256)
         part = lax.dot_general(
-            ug[yy[e], :, :, cols].reshape(512, 256), ag[yy[e]], (((0,), (0,)), ((), ())),
+            tokens(e)[:, :, cols].reshape(512, 256), ag[yy[e], :, act_cols], (((0,), (0,)), ((), ())),
             preferred_element_type=F32,
-        ).reshape(2, 128, 1024)
+        ).reshape(2, 128, CA)
         here = pl.ds(2 * m, 2)
         acc[here] = acc[here] + part
 
@@ -411,12 +442,50 @@
             gs[k, s, here, :] = acc[target, here, :].astype(BF)
         send(grad_id(k, s, half), gs.at[k, s, here], gr.at[k, s, here], z=zz[1] if k == 0 else zz[7])
 
-    top, bottom = pl.ds(0, 256), pl.ds(256, 256)
+    def side_part(e):
+        quarter = up[e].reshape(512, 1024)
+        part = lax.dot_general(
+            ag[y, :, pl.ds(CA, CW)], quarter, (((0,), (0,)), ((), ())), preferred_element_type=F32
+        ).astype(BF)
+        for k in range(8):
+            gp[k, e] = part[:, k * 128 : (k + 1) * 128]
+
+    def side_id(k, s, half):
+        return GOS + (k * 4 + s) * 2 + half
+
+    def side_send(k, s, half, add):
+        target = zz[4 - s] if k == 0 else zz[4 + s]
+        here = pl.ds(half * 2, 2)
+        if add:
+            arrived(side_id(k, s - 1, half), gq.at[k, s - 1, here], z=zz[7] if k == 0 else zz[1])
+            gp[target, here] = (gp[target, here].astype(F32) + gq[k, s - 1, here].astype(F32)).astype(BF)
+        send(side_id(k, s, half), gp.at[target, here], gq.at[k, s, here], z=zz[1] if k == 0 else zz[7])
+
+    def side_sum():
+        for half in (0, 1):
+            here = pl.ds(half * 2, 2)
+            for k in range(2):
+                arrived(side_id(k, 3, half), gq.at[k, 3, here], z=zz[7] if k == 0 else zz[1])
+            total = gp[z, here].astype(F32) + gq[0, 3, here].astype(F32) + gq[1, 3, here].astype(F32)
+            gp[z, here] = total.astype(BF)
+        for d in (2, 1, 3):
+            send(GYS + d, gp.at[z, d], gy.at[d - 1], y=yy[d])
+
+    def side_last():
+        for d in (1, 2, 3):
+            arrived(GYS + d, gy.at[d - 1], y=yy[4 - d])
+        total = gp[z, 0].astype(F32)
+        for d in range(3):
+            total = total + gy[d].astype(F32)
+        go[:, pl.ds(CA, CW)] = total.T * (1.0 / 32.0)
+
+    top, bottom = pl.ds(0, TOP), pl.ds(TOP, 512 - TOP)
+    hh_rows = (pl.ds(0, TOP), pl.ds(0, 512 - TOP))
 
     def hidden_hop(k):
         slot, here = (0, top) if k == 0 else (2, bottom)
-        arrived(HHS + k, hh.at[k], y=yy[3] if k == 0 else yy[1])
-        start = 0 if k == 0 else 256
+        arrived(HHS + k, hh.at[k, hh_rows[k]], y=yy[3] if k == 0 else yy[1])
+        start, count = (0, TOP // 16) if k == 0 else (TOP, (512 - TOP) // 16)
 
         def rows(i, carry):
             there = pl.ds(pl.multiple_of(i * 16, 16), 16)
@@ -425,7 +494,7 @@
             hp[slot, mine, :] = total.astype(BF)
             return carry
 
-        lax.fori_loop(0, 16, rows, 0)
+        lax.fori_loop(0, count, rows, 0)
         send(HFS + 2 + k, hp.at[slot, here], hf.at[k, here], y=yy[1] if k == 0 else yy[3])
 
     main_cols = pl.ds(0, CQ)
@@ -436,7 +505,7 @@
             h0[here, main_cols] = h0[here, main_cols] + hf[k, here, :].astype(F32)
             return carry
 
-        lax.fori_loop(0, 16, rows, 0)
+        lax.fori_loop(0, (512 - TOP if start else TOP) // 16, rows, 0)
 
     def finish(k, start):
         def rows(i, carry):
@@ -445,65 +514,86 @@
             h0[here, main_cols] = total * slope_v[here, main_cols]
             return carry
 
-        lax.fori_loop(0, 16, rows, 0)
+        lax.fori_loop(0, (512 - TOP if start else TOP) // 16, rows, 0)
 
     gelu(0)
-    act_own(0)
+    to_others()
     gelu(1)
     gelu(2)
     gelu(3)
+    act_own(0)
     got_seg.wait()
     got_qkv.wait()
-    for pair in range(4):
-        attend(pair)
+    attend(0)
+    attend(1)
+    own_first(2)
+    own_first(3)
+    own_twin(0, t)
+    attend(2)
+    attend(3)
     weight_hop(1)
-    act_own(1)
+    side_own()
+    own_hop(0)
+    own_hop(1)
     got_ow.wait()
     lax.fori_loop(0, 3, project, 0)
-    side_own()
-    for e in (3, 1, 2):
-        own_upstream(e)
-    send(U2S, ug.at[:, t], ug.at[:, t], c=oc)
+    act_own(1)
+    own_hop(3)
+    own_hop(2)
+    own_twin(1, t_left)
+    own_twin(2, t_right)
     lax.fori_loop(3, 8, project, 0)
     for e in (2, 1, 3, 0):
         send(ATS + e, att_p.at[xx[e], oc], att_r.at[xx[e]], c=oc)
     act_hop(0)
     act_own(2)
+    for e in (3, 1, 2):
+        other_first(e)
+    other_twin(0, t)
     weight_hop(2)
-    upstream_hop(0)
-    upstream_hop(3)
     side_hop(1)
+    own_far()
+    own_twin(3, t_far)
     act_hop(1)
     act_own(3)
-    upstream_hop(1)
-    upstream_hop(2)
-    send(U2S + 1, ug.at[:, t_left], ug.at[:, t_left], c=oc)
-    send(U2S + 2, ug.at[:, t_right], ug.at[:, t_right], c=oc)
-    for e in (1, 3, 2):
-        others_own(e)
-    send(UOS, uo.at[:, t], uo.at[:, t], c=oc)
+    own_all()
+    for e in range(4):
+        side_part(e)
+    side_send(0, 0, 0, False)
+    side_send(1, 0, 1, False)
+    side_send(0, 1, 1, False)
+    side_send(1, 1, 0, False)
+    weight_part(0, True)
+    for e in (3, 1, 2):
+        other_hop(e)
+    other_twin(1, t_left)
+    other_twin(2, t_right)
     weight_hop(3)
+    act_hop(2)
     side_hop(2)
-    act_hop(2)
-    upstream_far()
-    send(U2S + 3, ug.at[:, t_far], ug.at[:, t_far], c=oc)
+    side_send(0, 1, 0, True)
+    side_send(1, 1, 1, True)
+    side_send(0, 2, 1, True)
+    side_send(1, 2, 0, True)
+    other_far()
+    other_twin(3, t_far)
     att_first()
-    for k, dx in ((0, 0), (1, 3), (2, 1), (3, 2)):
-        arrived(U2S + k, ug.at[:, 2 * xx[dx] + oc], c=oc)
-    weight_part(0, True)
+    act_hop(3)
     weight_far()
+    other_all()
     hidden(2, to_send(2))
+    send(HHS, hp.at[1, top], hh.at[0, hh_rows[0]], y=yy[1])
+    send(HHS + 1, hp.at[1, bottom], hh.at[1, hh_rows[1]], y=yy[3])
+    side_send(0, 2, 0, True)
+    side_send(1, 2, 1, True)
+    side_send(0, 3, 1, True)
+    side_send(1, 3, 0, True)
+    weight_part(3, False)
     side_hop(3)
-    act_hop(3)
-    send(HHS, hp.at[1, top], hh.at[0], y=yy[1])
-    send(HHS + 1, hp.at[1, bottom], hh.at[1], y=yy[3])
-    for e in (1, 3, 2):
-        others_hop(e)
-    send(UOS + 1, uo.at[:, t_left], uo.at[:, t_left], c=oc)
-    send(UOS + 2, uo.at[:, t_right], uo.at[:, t_right], c=oc)
-    weight_part(3, False)
     weight_part(1, False)
     att_second()
+    side_send(0, 3, 0, True)
+    side_send(1, 3, 1, True)
     act_far()
     weight_tile(2, 0)
     grad_send(0, 0, 0, False)
@@ -515,11 +605,9 @@
     send(HFS, hp.at[0, bottom], hf.at[0, bottom], y=yy[1])
     hidden(3, to_send(3))
     send(HFS + 1, hp.at[2, top], hf.at[1, top], y=yy[3])
-    others_far()
-    send(UOS + 3, uo.at[:, t_far], uo.at[:, t_far], c=oc)
-    side_far()
     grad_send(0, 1, 0, True)
     grad_send(1, 1, 1, True)
+    side_sum()
     grad_send(0, 2, 1, True)
     grad_send(1, 2, 0, True)
     hidden_hop(0)
@@ -527,18 +615,18 @@
     hidden(0, to_keep)
     grad_send(0, 2, 0, True)
     grad_send(1, 2, 1, True)
+    side_far()
+    hidden_side()
     grad_send(0, 3, 1, True)
     grad_send(1, 3, 0, True)
-    for k, dx in ((0, 0), (1, 3), (2, 1), (3, 2)):
-        arrived(UOS + k, uo.at[:, 2 * xx[dx] + oc], c=oc)
-    hidden_side()
     grad_send(0, 3, 0, True)
     grad_send(1, 3, 1, True)
+    side_last()
     att_last()
 
     arrived(HFS, hf.at[0, bottom], y=yy[3])
     arrived(HFS + 1, hf.at[1, top], y=yy[1])
-    fold(0, 256)
+    fold(0, TOP)
     fold(1, 0)
 
     def grad_last(half):
@@ -546,31 +634,43 @@
         for k in range(2):
             arrived(grad_id(k, 3, half), gr.at[k, 3, here], z=zz[7] if k == 0 else zz[1])
         total = acc[z, here, :] + gr[0, 3, here, :].astype(F32) + gr[1, 3, here, :].astype(F32)
-        go[here, :] = total * (1.0 / 32.0)
+        go[here, act_cols] = total * (1.0 / 32.0)
 
     grad_last(0)
     grad_last(1)
     arrived(HFS + 2, hf.at[0, top], y=yy[3])
     finish(0, 0)
     arrived(HFS + 3, hf.at[1, bottom], y=yy[1])
-    finish(1, 256)
-
-    for copy in sent:
+    finish(1, TOP)
+
+    for copy in sent[-N_SEND:]:
         copy.wait_send()
+    assert len(place) == N_IDS, len(place)
+
+
+def put(a, b, c, a_out, b_out, c_out, sem):
+    copies = []
+    for k, (src, dst) in enumerate(((b, b_out), (a, a_out), (c, c_out))):
+        copies.append(pltpu.make_async_copy(src, dst, sem.at[k]))
+        copies[-1].start()
+    for copy in copies:
+        copy.wait()
 
 
 def body(*args):
     hbm = pl.BlockSpec(memory_space=pltpu.HBM)
     vmem = pltpu.VMEM
-    return pl.pallas_call(
+    in_vmem = (pl.BlockSpec(memory_space=pltpu.VMEM),) * 3
+    shapes = (
+        jax.ShapeDtypeStruct((64, 4096), F32),
+        jax.ShapeDtypeStruct((512, 1024), F32),
+        jax.ShapeDtypeStruct((128, 1024), F32),
+    )
+    parts = pl.pallas_call(
         kernel,
-        out_shape=(
-            jax.ShapeDtypeStruct((64, 4096), F32),
-            jax.ShapeDtypeStruct((512, 1024), F32),
-            jax.ShapeDtypeStruct((128, 1024), F32),
-        ),
+        out_shape=shapes,
         in_specs=[hbm] * 7,
-        out_specs=(pl.BlockSpec(memory_space=pltpu.VMEM),) * 3,
+        out_specs=in_vmem,
         scratch_shapes=[
             vmem((3, 512, 512), BF),
             vmem((1, 8, 64), jnp.int32),
@@ -589,12 +689,15 @@
             vmem((2, 64, 2048), BF),
             vmem((2, 64, 4096), BF),
             vmem((3, 512, CQ), BF),
-            vmem((2, 256, CQ), BF),
+            vmem((2, TOP, CQ), BF),
             vmem((2, 512, CQ), BF),
-            vmem((8, 128, 1024), F32),
-            vmem((2, 4, 128, 1024), BF),
-            vmem((2, 4, 128, 1024), BF),
-            pltpu.SemaphoreType.DMA((N_IDS,)),
+            vmem((8, 128, CA), F32),
+            vmem((2, 4, 128, CA), BF),
+            vmem((2, 4, 128, CA), BF),
+            vmem((8, 4, CW, 128), BF),
+            vmem((2, 4, 4, CW, 128), BF),
+            vmem((3, CW, 128), BF),
+            pltpu.SemaphoreType.DMA((N_SEND,)),
             pltpu.SemaphoreType.DMA((N_IDS,)),
             pltpu.SemaphoreType.DMA((N_LOCAL,)),
         ],
@@ -603,6 +706,15 @@
         ),
         name="layer",
     )(*(pltpu.with_memory_space_constraint(a, pltpu.HBM) for a in args))
+    return pl.pallas_call(
+        put,
+        out_shape=shapes,
+        in_specs=in_vmem,
+        out_specs=(hbm,) * 3,
+        scratch_shapes=[pltpu.SemaphoreType.DMA((3,))],
+        compiler_params=pltpu.CompilerParams(vmem_limit_bytes=1 * 1024 * 1024),
+        name="put",
+    )(*parts)
 
 
 def solution(mesh):

time: 85.1 us -> 81 us (0.952)
  local copies, waits for them, and re-layouts: 3.08 us -> 0 us
  Pallas kernels: 80.3 us -> 79.3 us
    unnamed x3 -> x0, local copies, waits for them, and re-layouts: 3.08 us -> none
    pallas_call x1 -> x2, Pallas kernels: 80.3 us -> 79.3 us  [the longest x1 77.5 us: body(): pl.pallas_call(kernel, out_shape=shapes, in_specs=[hbm] * 7, out_specs=in...]
where the time goes in v3:
time: 81 us; the launch traced here: 80 us
  Pallas kernels  79.3 us (98%)
    pallas_call x1, Pallas kernels, body(): pl.pallas_call(kernel, out_shape=shapes, in_specs=[hbm] * 7, out_specs=in...  77.5 us
    pallas_call x1, Pallas kernels, body(): pl.pallas_call(put, out_shape=shapes, in_specs=in_vmem, out_specs=(hbm,)...  1.86 us

profile of v3, /device:TPU:1, one launch (start us, length us, event | category | flops | bytes accessed | tf_op | source)
XLA Modules:
  0.0 80.0 jit_solution(569977672084589277)
XLA Ops:
  0.6 77.5 %layer.1 = (f32[64,4096]{1,0:T(8,128)S(1)}, f32[512,1024]{1,0:T(8,128)S(1)}, f32[128,1024]{1,0:T(8,128)S(1)}) custom-call(bf16[3,512,512]{2,1,0:T(8,128)(2,1)} %qkv.1, s32[1,8,64]{2,1,0:T(8,128)} %seg.1, bf16[4096,512]{1,0:T(8,128)(2,1)} %out_weight.1, bf16[4096]{0:T(1024)(128)(2,1)} %bias.1, bf16[64,4096]{1,0:T(8,128)(2,1)} %upstream.1, ...), custom_call_target="tpu_custom_call" | custom-call | tf_op jit(solution)/shard_map/layer/pallas_call | solution.py:669
  78.1 1.9 %put.1 = (f32[64,4096]{1,0:T(8,128)}, f32[512,1024]{1,0:T(8,128)}, f32[128,1024]{1,0:T(8,128)}) custom-call(f32[64,4096]{1,0:T(8,128)S(1)} %get-tuple-element.6.a, f32[512,1024]{1,0:T(8,128)S(1)} %get-tuple-element.7.b, f32[128,1024]{1,0:T(8,128)S(1)} %get-tuple-element.8.c), custom_call_target="tpu_custom_call" | custom-call | tf_op jit(solution)/shard_map/put/pallas_call | solution.py:709

commit v4 on v3

--- a/solution.py
+++ b/solution.py
@@ -49,7 +49,7 @@
 GOS = IDS.take(16)
 GYS = IDS.take(4)
 N_IDS = 109
-N_SEND = 40
+N_SEND = 28
 
 LOCAL = Ids()
 L_QKV, L_SEG, L_OW, L_PRE, L_W, L_BIAS = (LOCAL.take() for _ in range(6))
@@ -60,7 +60,7 @@
 CQ = 1024 - CO
 CW = 128
 CA = 1024 - CW
-TOP = 288
+TOP = 240
 
 
 def kernel(
@@ -127,7 +127,7 @@
     send(WR, wg.at[z], wg.at[z], z=zz[1])
     send(WL, wg.at[z], wg.at[z], z=zz[7])
     for d in (1, 3, 2):
-        send(WY + d, wg.at[z, :, pl.ds(CQ, CO)], wo.at[3 - d, z], y=yy[d])
+        send(WY, wg.at[z, :, pl.ds(CQ, CO)], wo.at[3 - d, z], y=yy[d])
 
     for copy in got_up:
         copy.wait()
@@ -163,22 +163,18 @@
         send(AL + q, mine, mine, y=yy[3])
 
     def act_hop(q):
-        part = pl.ds(q * 128, 128)
-        low_slot, high_slot = ag.at[yy[3], part, act_cols], ag.at[yy[1], part, act_cols]
-        arrived(AR + q, low_slot, y=yy[3])
-        if q % 2 == 0:
-            send(ARF + q, low_slot, low_slot, y=yy[1])
-        arrived(AL + q, high_slot, y=yy[1])
-        if q % 2 == 1:
-            send(ALF + q, high_slot, high_slot, y=yy[3])
+        below, above = yy[3], yy[1]
+        part, half = pl.ds(q * 128, 128), pl.ds(q * 128, 64)
+        arrived(AR + q, ag.at[below, part, act_cols], y=below)
+        send(ARF + q, ag.at[below, half, act_cols], ag.at[below, half, act_cols], y=above)
+        half = pl.ds(q * 128 + 64, 64)
+        arrived(AL + q, ag.at[above, part, act_cols], y=above)
+        send(ALF + q, ag.at[above, half, act_cols], ag.at[above, half, act_cols], y=below)
 
     def act_far():
         for q in range(4):
-            slot = ag.at[yy[2], pl.ds(q * 128, 128), act_cols]
-            if q % 2 == 0:
-                arrived(ARF + q, slot, y=yy[3])
-            else:
-                arrived(ALF + q, slot, y=yy[1])
+            arrived(ARF + q, ag.at[yy[2], pl.ds(q * 128, 64), act_cols], y=yy[3])
+            arrived(ALF + q, ag.at[yy[2], pl.ds(q * 128 + 64, 64), act_cols], y=yy[1])
 
     t_left, t_right, t_far = 2 * xx[3] + c, 2 * xx[1] + c, 2 * xx[2] + c
     first, last = pl.ds(0, 32), pl.ds(32, 32)
@@ -186,16 +182,16 @@
     def own_hop(e):
         left, right = up.at[e, t_left], up.at[e, t_right]
         arrived(UPR + e, left, x=xx[3])
-        if e in (0, 1):
+        if e in (0, 2):
             send(UPFR + e, left, left, x=xx[1])
         arrived(UPL + e, right, x=xx[1])
-        if e in (2, 3):
+        if e in (1, 3):
             send(UPFL + e, right, right, x=xx[3])
 
     def own_far():
-        for e in (0, 1):
+        for e in (0, 2):
             arrived(UPFR + e, up.at[e, t_far], x=xx[3])
-        for e in (2, 3):
+        for e in (1, 3):
             arrived(UPFL + e, up.at[e, t_far], x=xx[1])
 
     def other_first(e):
@@ -257,8 +253,7 @@
         arrived(WL + 3, wg.at[zz[4], high], z=zz[1])
 
     def side_own():
-        for e in (1, 3, 2):
-            arrived(WY + 4 - e, wo.at[e - 1, z], y=yy[e])
+        arrived(WY, wo.at[:, z], y=yy[1])
         send(WOR, wo.at[:, z], wo.at[:, z], z=zz[1])
         send(WOL, wo.at[:, z], wo.at[:, z], z=zz[7])
 
@@ -361,8 +356,8 @@
         lax.fori_loop(0, 4, att_rows, 0)
 
     def hidden(d, store):
-        def tile(n, carry):
-            cols = pl.ds(pl.multiple_of(n * 256, 256), 256)
+        for start in range(0, CQ, 256):
+            cols = pl.ds(start, 256)
             store(
                 cols,
                 jnp.dot(
@@ -370,9 +365,6 @@
                     preferred_element_type=F32,
                 ),
             )
-            return carry
-
-        lax.fori_loop(0, CQ // 256, tile, 0)
 
     def to_send(d):
         def store(cols, value):
@@ -469,11 +461,10 @@
             total = gp[z, here].astype(F32) + gq[0, 3, here].astype(F32) + gq[1, 3, here].astype(F32)
             gp[z, here] = total.astype(BF)
         for d in (2, 1, 3):
-            send(GYS + d, gp.at[z, d], gy.at[d - 1], y=yy[d])
+            send(GYS, gp.at[z, d], gy.at[d - 1], y=yy[d])
 
     def side_last():
-        for d in (1, 2, 3):
-            arrived(GYS + d, gy.at[d - 1], y=yy[4 - d])
+        arrived(GYS, gy, y=yy[1])
         total = gp[z, 0].astype(F32)
         for d in range(3):
             total = total + gy[d].astype(F32)
@@ -516,69 +507,74 @@
 
         lax.fori_loop(0, (512 - TOP if start else TOP) // 16, rows, 0)
 
+    own_first(2)
     gelu(0)
+    gelu(3)
     to_others()
+    act_own(0)
+    side_own()
+    gelu(2)
+    own_first(3)
     gelu(1)
-    gelu(2)
-    gelu(3)
-    act_own(0)
+    weight_hop(1)
+    own_twin(0, t)
+    own_hop(1)
+    own_hop(2)
+    own_hop(0)
     got_seg.wait()
     got_qkv.wait()
-    attend(0)
-    attend(1)
-    own_first(2)
-    own_first(3)
-    own_twin(0, t)
-    attend(2)
     attend(3)
-    weight_hop(1)
-    side_own()
-    own_hop(0)
-    own_hop(1)
-    got_ow.wait()
-    lax.fori_loop(0, 3, project, 0)
+    side_hop(1)
     act_own(1)
     own_hop(3)
-    own_hop(2)
+    attend(1)
+    attend(0)
+    act_own(2)
+    other_first(3)
+    attend(2)
     own_twin(1, t_left)
+    weight_hop(2)
+    other_first(2)
+    got_ow.wait()
+    lax.fori_loop(0, 1, project, 0)
+    act_own(3)
+    own_far()
+    other_first(1)
     own_twin(2, t_right)
-    lax.fori_loop(3, 8, project, 0)
-    for e in (2, 1, 3, 0):
-        send(ATS + e, att_p.at[xx[e], oc], att_r.at[xx[e]], c=oc)
-    act_hop(0)
-    act_own(2)
-    for e in (3, 1, 2):
-        other_first(e)
-    other_twin(0, t)
-    weight_hop(2)
-    side_hop(1)
-    own_far()
+    lax.fori_loop(1, 2, project, 0)
     own_twin(3, t_far)
-    act_hop(1)
-    act_own(3)
+    lax.fori_loop(2, 6, project, 0)
     own_all()
+    lax.fori_loop(6, 7, project, 0)
     for e in range(4):
         side_part(e)
     side_send(0, 0, 0, False)
     side_send(1, 0, 1, False)
     side_send(0, 1, 1, False)
     side_send(1, 1, 0, False)
+    other_hop(3)
+    other_twin(0, t)
+    lax.fori_loop(7, 8, project, 0)
     weight_part(0, True)
-    for e in (3, 1, 2):
-        other_hop(e)
+    other_hop(2)
+    act_hop(0)
+    other_hop(1)
+    act_hop(1)
+    for e in (2, 1, 3, 0):
+        send(ATS + e, att_p.at[xx[e], oc], att_r.at[xx[e]], c=oc)
+    weight_hop(3)
     other_twin(1, t_left)
-    other_twin(2, t_right)
-    weight_hop(3)
     act_hop(2)
-    side_hop(2)
     side_send(0, 1, 0, True)
     side_send(1, 1, 1, True)
+    act_hop(3)
+    att_first()
+    other_twin(2, t_right)
+    side_hop(2)
     side_send(0, 2, 1, True)
     side_send(1, 2, 0, True)
     other_far()
     other_twin(3, t_far)
-    att_first()
-    act_hop(3)
     weight_far()
     other_all()
     hidden(2, to_send(2))
@@ -586,48 +582,47 @@
     send(HHS + 1, hp.at[1, bottom], hh.at[1, hh_rows[1]], y=yy[3])
     side_send(0, 2, 0, True)
     side_send(1, 2, 1, True)
+    weight_part(3, False)
+    weight_part(1, False)
+    act_far()
+    side_hop(3)
+    weight_tile(2, 0)
+    grad_send(0, 0, 0, False)
+    grad_send(1, 0, 1, False)
+    hidden(3, to_send(3))
+    send(HFS + 1, hp.at[2, top], hf.at[1, top], y=yy[3])
     side_send(0, 3, 1, True)
     side_send(1, 3, 0, True)
-    weight_part(3, False)
-    side_hop(3)
-    weight_part(1, False)
+    hidden(1, to_send(1))
+    send(HFS, hp.at[0, bottom], hf.at[0, bottom], y=yy[1])
+    lax.fori_loop(1, 4, lambda i, carry: weight_tile(2, i), None)
+    side_far()
     att_second()
     side_send(0, 3, 0, True)
     side_send(1, 3, 1, True)
-    act_far()
-    weight_tile(2, 0)
-    grad_send(0, 0, 0, False)
-    grad_send(1, 0, 1, False)
-    lax.fori_loop(1, 4, lambda i, carry: weight_tile(2, i), None)
     grad_send(0, 1, 1, False)
     grad_send(1, 1, 0, False)
-    hidden(1, to_send(1))
-    send(HFS, hp.at[0, bottom], hf.at[0, bottom], y=yy[1])
-    hidden(3, to_send(3))
-    send(HFS + 1, hp.at[2, top], hf.at[1, top], y=yy[3])
     grad_send(0, 1, 0, True)
     grad_send(1, 1, 1, True)
     side_sum()
-    grad_send(0, 2, 1, True)
-    grad_send(1, 2, 0, True)
     hidden_hop(0)
     hidden_hop(1)
     hidden(0, to_keep)
+    grad_send(0, 2, 1, True)
+    grad_send(1, 2, 0, True)
     grad_send(0, 2, 0, True)
     grad_send(1, 2, 1, True)
-    side_far()
-    hidden_side()
+    arrived(HFS, hf.at[0, bottom], y=yy[3])
+    fold(0, TOP)
+    arrived(HFS + 1, hf.at[1, top], y=yy[1])
+    fold(1, 0)
+    side_last()
     grad_send(0, 3, 1, True)
     grad_send(1, 3, 0, True)
+    hidden_side()
     grad_send(0, 3, 0, True)
     grad_send(1, 3, 1, True)
-    side_last()
     att_last()
-
-    arrived(HFS, hf.at[0, bottom], y=yy[3])
-    arrived(HFS + 1, hf.at[1, top], y=yy[1])
-    fold(0, TOP)
-    fold(1, 0)
 
     def grad_last(half):
         here = pl.ds(half * 64, 64)
@@ -650,8 +645,10 @@
 
 def put(a, b, c, a_out, b_out, c_out, sem):
     copies = []
-    for k, (src, dst) in enumerate(((b, b_out), (a, a_out), (c, c_out))):
-        copies.append(pltpu.make_async_copy(src, dst, sem.at[k]))
+    pieces = [(b, b_out, i * 128, 128) for i in range(4)] + [(a, a_out, i * 16, 16) for i in range(4)]
+    for k, (src, dst, start, rows) in enumerate(pieces + [(c, c_out, 0, 128)]):
+        here = pl.ds(start, rows)
+        copies.append(pltpu.make_async_copy(src.at[here], dst.at[here], sem.at[k]))
         copies[-1].start()
     for copy in copies:
         copy.wait()
@@ -689,7 +686,7 @@
             vmem((2, 64, 2048), BF),
             vmem((2, 64, 4096), BF),
             vmem((3, 512, CQ), BF),
-            vmem((2, TOP, CQ), BF),
+            vmem((2, max(TOP, 512 - TOP), CQ), BF),
             vmem((2, 512, CQ), BF),
             vmem((8, 128, CA), F32),
             vmem((2, 4, 128, CA), BF),
@@ -711,7 +708,7 @@
         out_shape=shapes,
         in_specs=in_vmem,
         out_specs=(hbm,) * 3,
-        scratch_shapes=[pltpu.SemaphoreType.DMA((3,))],
+        scratch_shapes=[pltpu.SemaphoreType.DMA((9,))],
         compiler_params=pltpu.CompilerParams(vmem_limit_bytes=1 * 1024 * 1024),
         name="put",
     )(*parts)

time: 81 us -> 79 us (0.975); the launches traced: 80 us -> 78.9 us
  Pallas kernels: 79.3 us -> 78.3 us
    pallas_call x1, Pallas kernels: 77.5 us -> 76.3 us  [body(): pl.pallas_call(kernel, out_shape=shapes, in_specs=[hbm] * 7, out_specs=in...]
where the time goes in v4:
time: 79 us; the launch traced here: 78.9 us
  Pallas kernels  78.3 us (99%)
    pallas_call x1, Pallas kernels, body(): pl.pallas_call(kernel, out_shape=shapes, in_specs=[hbm] * 7, out_specs=in...  76.3 us
    pallas_call x1, Pallas kernels, body(): pl.pallas_call(put, out_shape=shapes, in_specs=in_vmem, out_specs=(hbm,)...  1.91 us

profile of v4, /device:TPU:1, one launch (start us, length us, event | category | flops | bytes accessed | tf_op | source)
XLA Modules:
  0.0 78.9 jit_solution(17200668206622120628)
XLA Ops:
  0.6 76.3 %layer.1 = (f32[64,4096]{1,0:T(8,128)S(1)}, f32[512,1024]{1,0:T(8,128)S(1)}, f32[128,1024]{1,0:T(8,128)S(1)}) custom-call(bf16[3,512,512]{2,1,0:T(8,128)(2,1)} %qkv.1, s32[1,8,64]{2,1,0:T(8,128)} %seg.1, bf16[4096,512]{1,0:T(8,128)(2,1)} %out_weight.1, bf16[4096]{0:T(1024)(128)(2,1)} %bias.1, bf16[64,4096]{1,0:T(8,128)(2,1)} %upstream.1, ...), custom_call_target="tpu_custom_call" | custom-call | tf_op jit(solution)/shard_map/layer/pallas_call | solution.py:666
  77.0 1.9 %put.1 = (f32[64,4096]{1,0:T(8,128)}, f32[512,1024]{1,0:T(8,128)}, f32[128,1024]{1,0:T(8,128)}) custom-call(f32[64,4096]{1,0:T(8,128)S(1)} %get-tuple-element.6.a, f32[512,1024]{1,0:T(8,128)S(1)} %get-tuple-element.7.b, f32[128,1024]{1,0:T(8,128)S(1)} %get-tuple-element.8.c), custom_call_target="tpu_custom_call" | custom-call | tf_op jit(solution)/shard_map/put/pallas_call | solution.py:706

commit v5 on v4

--- a/solution.py
+++ b/solution.py
@@ -48,12 +48,12 @@
 GRS = IDS.take(16)
 GOS = IDS.take(16)
 GYS = IDS.take(4)
-N_IDS = 109
-N_SEND = 28
+N_IDS = 105
+N_SEND = 22
 
 LOCAL = Ids()
 L_QKV, L_SEG, L_OW, L_PRE, L_W, L_BIAS = (LOCAL.take() for _ in range(6))
-L_UP = LOCAL.take(4)
+L_UP = LOCAL.take()
 N_LOCAL = LOCAL.n
 
 CO = 256
@@ -105,10 +105,16 @@
         copy.start()
         return copy
 
+    barrier = pltpu.get_barrier_semaphore()
+    peers = [{"y": yy[d]} for d in (1, 2, 3)] + [{"z": zz[d]} for d in (1, 7)]
+    peers += [{"x": xx[d]} for d in (1, 3)] + [{"c": oc}]
+    for peer in peers:
+        pl.semaphore_signal(barrier, inc=1, device_id=peer, device_id_type=pl.DeviceIdType.MESH)
+
     got_pre = fetch(L_PRE, pre_act, pre_v)
     got_w = fetch(L_W, down_weight, wg.at[z])
     got_up = [
-        fetch(L_UP + e, upstream.at[:, pl.ds(pl.multiple_of(yy[e] * 1024, 1024), 1024)], up.at[e, t])
+        fetch(L_UP, upstream.at[:, pl.ds(pl.multiple_of(yy[e] * 1024, 1024), 1024)], up.at[e, t])
         for e in range(4)
     ]
     got_seg = fetch(L_SEG, seg, seg_v)
@@ -116,11 +122,6 @@
     got_bias = fetch(L_BIAS, bias, bias_v)
     got_ow = fetch(L_OW, out_weight, ow_v)
 
-    barrier = pltpu.get_barrier_semaphore()
-    peers = [{"y": yy[d]} for d in (1, 2, 3)] + [{"z": zz[d]} for d in (1, 7)]
-    peers += [{"x": xx[d]} for d in (1, 3)] + [{"c": oc}]
-    for peer in peers:
-        pl.semaphore_signal(barrier, inc=1, device_id=peer, device_id_type=pl.DeviceIdType.MESH)
     pl.semaphore_wait(barrier, len(peers))
 
     got_w.wait()
@@ -129,8 +130,7 @@
     for d in (1, 3, 2):
         send(WY, wg.at[z, :, pl.ds(CQ, CO)], wo.at[3 - d, z], y=yy[d])
 
-    for copy in got_up:
-        copy.wait()
+    pltpu.make_async_copy(up.at[:, t], up.at[:, t], lsem.at[L_UP]).wait()
 
     def own_first(e):
         send(UPR + e, up.at[e, t], up.at[e, t], x=xx[1])
@@ -164,17 +164,22 @@
 
     def act_hop(q):
         below, above = yy[3], yy[1]
-        part, half = pl.ds(q * 128, 128), pl.ds(q * 128, 64)
-        arrived(AR + q, ag.at[below, part, act_cols], y=below)
-        send(ARF + q, ag.at[below, half, act_cols], ag.at[below, half, act_cols], y=above)
-        half = pl.ds(q * 128 + 64, 64)
-        arrived(AL + q, ag.at[above, part, act_cols], y=above)
-        send(ALF + q, ag.at[above, half, act_cols], ag.at[above, half, act_cols], y=below)
+        part = pl.ds(q * 128, 128)
+        low_slot, high_slot = ag.at[below, part, act_cols], ag.at[above, part, act_cols]
+        arrived(AR + q, low_slot, y=below)
+        if q % 2 == 0:
+            send(ARF + q, low_slot, low_slot, y=above)
+        arrived(AL + q, high_slot, y=above)
+        if q % 2 == 1:
+            send(ALF + q, high_slot, high_slot, y=below)
 
     def act_far():
         for q in range(4):
-            arrived(ARF + q, ag.at[yy[2], pl.ds(q * 128, 64), act_cols], y=yy[3])
-            arrived(ALF + q, ag.at[yy[2], pl.ds(q * 128 + 64, 64), act_cols], y=yy[1])
+            slot = ag.at[yy[2], pl.ds(q * 128, 128), act_cols]
+            if q % 2 == 0:
+                arrived(ARF + q, slot, y=yy[3])
+            else:
+                arrived(ALF + q, slot, y=yy[1])
 
     t_left, t_right, t_far = 2 * xx[3] + c, 2 * xx[1] + c, 2 * xx[2] + c
     first, last = pl.ds(0, 32), pl.ds(32, 32)

time: 79 us -> 78.8 us (level)
  no operation moved by 1% of the time
where the time goes in v5:
time: 78.8 us; the launch traced here: 78.7 us
  Pallas kernels  78.1 us (99%)
    pallas_call x1, Pallas kernels, body(): pl.pallas_call(kernel, out_shape=shapes, in_specs=[hbm] * 7, out_specs=in...  76.2 us
    pallas_call x1, Pallas kernels, body(): pl.pallas_call(put, out_shape=shapes, in_specs=in_vmem, out_specs=(hbm,)...  1.91 us

profile of v5, /device:TPU:1, one launch (start us, length us, event | category | flops | bytes accessed | tf_op | source)
XLA Modules:
  0.0 78.7 jit_solution(14140576924514895345)
XLA Ops:
  0.6 76.2 %layer.1 = (f32[64,4096]{1,0:T(8,128)S(1)}, f32[512,1024]{1,0:T(8,128)S(1)}, f32[128,1024]{1,0:T(8,128)S(1)}) custom-call(bf16[3,512,512]{2,1,0:T(8,128)(2,1)} %qkv.1, s32[1,8,64]{2,1,0:T(8,128)} %seg.1, bf16[4096,512]{1,0:T(8,128)(2,1)} %out_weight.1, bf16[4096]{0:T(1024)(128)(2,1)} %bias.1, bf16[64,4096]{1,0:T(8,128)(2,1)} %upstream.1, ...), custom_call_target="tpu_custom_call" | custom-call | tf_op jit(solution)/shard_map/layer/pallas_call | solution.py:671
  76.8 1.9 %put.1 = (f32[64,4096]{1,0:T(8,128)}, f32[512,1024]{1,0:T(8,128)}, f32[128,1024]{1,0:T(8,128)}) custom-call(f32[64,4096]{1,0:T(8,128)S(1)} %get-tuple-element.6.a, f32[512,1024]{1,0:T(8,128)S(1)} %get-tuple-element.7.b, f32[128,1024]{1,0:T(8,128)S(1)} %get-tuple-element.8.c), custom_call_target="tpu_custom_call" | custom-call | tf_op jit(solution)/shard_map/put/pallas_call | solution.py:711
